TPU v7x, 128 devices: a whole 4x4x4 slice. The times are simulated.
128 devices in a mesh: section: 8 (over y, x_hi), vocab: 16 (over z, x_lo, core).
Axes of the slice: x: 4 (x_hi: 2, x_lo: 2; x = x_hi * 2 + x_lo), y: 4, z: 4, core: 2. Of those that a mesh axis runs over, the one named last changes fastest.
Arguments:
- exit_hidden: bfloat16 [3, 256, 8192], P(None, 'vocab', 'section')
- norm_gain: float32 [3, 8192], P(None, 'section'), may hold values from 0.5 to 1.5
- head_weight: bfloat16 [8192, 65536], P(None, ('section', 'vocab'))
- teacher: float32 [256, 65536], P('vocab', 'section'), as said below
Outputs:
- divergence: float32 [3], replicated
- grad_hidden: bfloat16 [3, 256, 8192], P(None, 'vocab', 'section')
- grad_head: bfloat16 [8192, 65536], P(None, ('section', 'vocab'))
Inputs may be any that keep to these rules, and one draw needn't show every extreme that they name: Each row of teacher holds log-probabilities: their exponentials sum to one.
All inputs are finite; a program needn't handle non-finite values.
Results may differ from a plain program's by a relative error of at most 0.0086.
Values may be sent and summed in bfloat16 or wider, within the bound.
A program may use at most 128 MiB of HBM per device.

v0:
```python
import jax
import jax.numpy as jnp
from jax import lax
from jax.sharding import Mesh
from jax.sharding import PartitionSpec as P

D = 8192
TOK = 256
SECTION = ("section_0", "section_1")
VOCAB = ("vocab_0", "vocab_1", "vocab_2")
SECTION_VOCAB = ("section_0", "section_1", "vocab_0", "vocab_1", "vocab_2")


epsilon = 1e-05
loss_scale = 1024.0


def gathered_once(value, axis):
    leaves = jax.tree.leaves(value)
    turns = sorted(range(len(leaves)), key=lambda k: -leaves[k].size)
    width = (1, *leaves[turns[0]].shape)[-1]
    lines = [
        jnp.pad(leaves[k].reshape(-1), (0, -leaves[k].size % width)).reshape(-1, width)
        for k in turns
    ]
    both, at, found = (lax.all_gather(jnp.concatenate(lines), axis), 0, {})
    for k, line in zip(turns, lines):
        section = both[:, at : at + len(line)].reshape(len(both), -1)
        found[k] = section[:, : leaves[k].size].reshape(-1, *leaves[k].shape)
        at += len(line)
    numbers = iter(range(len(leaves)))
    return jax.tree.map(lambda _: found[next(numbers)], value)


def merged_by_axis(value, axes, combine):
    for axis in axes:
        pieces = gathered_once(value, axis)
        value = jax.tree.map(lambda part: part[0], pieces)
        for k in range(1, lax.axis_size(axis)):
            value = combine(value, jax.tree.map(lambda part: part[k], pieces))
    return value


def cut_along(value, dim, length):
    dims = value.shape
    parts = value.reshape(*dims[:dim], length, dims[dim] // length, *dims[dim + 1 :])
    return jnp.moveaxis(parts, dim, 0)


def sum_at_owner(value, axis, dim):
    length = lax.axis_size(axis)
    parts = lax.all_to_all(cut_along(value, dim, length), axis, 0, 0, tiled=True)
    return jnp.sum(parts, axis=0)


def combine(first, second):
    row_max = jnp.maximum(first[0], second[0])
    exp_total = first[1] * jnp.exp(first[0] - row_max) + second[1] * jnp.exp(second[0] - row_max)
    return (row_max, exp_total, first[2] + second[2], first[3] + second[3])


def body(exit_hidden, norm_gain, head_weight, teacher):
    hidden = exit_hidden.astype(jnp.float32)
    gains = norm_gain[:, None, :]
    squares = lax.psum(jnp.sum(hidden * hidden, axis=-1), SECTION)
    inverse = lax.rsqrt(squares / D + epsilon)[..., None]
    normed = (hidden * inverse * gains).astype(jnp.bfloat16)
    teacher_cols = lax.all_to_all(teacher, VOCAB, split_axis=1, concat_axis=0, tiled=True)
    token_full = lax.all_gather(normed, VOCAB, axis=1, tiled=True)
    gathered = lax.all_gather(token_full, SECTION, axis=2, tiled=True)
    exits_count = gathered.shape[0]
    tokens_count = gathered.shape[1]
    flat_rows = gathered.reshape(exits_count * tokens_count, D)
    local_vocab = head_weight.shape[1]
    logits = jnp.dot(flat_rows, head_weight, preferred_element_type=jnp.float32).reshape(
        exits_count, tokens_count, local_vocab
    )
    target = jnp.exp(teacher_cols)[None]
    cross_local = jnp.sum(target * (teacher_cols[None] - logits), axis=-1)
    weight_local = jnp.sum(target, axis=-1)
    local_max = jnp.max(logits, axis=-1)
    local_total = jnp.sum(jnp.exp(logits - local_max[..., None]), axis=-1)
    row_max, exp_total, cross, weight_sum = merged_by_axis(
        (local_max, local_total, cross_local, weight_local), SECTION_VOCAB, combine
    )
    log_total = row_max + jnp.log(exp_total)
    divergence = jnp.mean(cross + log_total * weight_sum, axis=-1)
    dlogit = ((jnp.exp(logits - log_total[..., None]) - target) * (loss_scale / TOK)).astype(
        jnp.bfloat16
    )
    flat_dlogit = dlogit.reshape(exits_count * tokens_count, local_vocab)
    grad_head = lax.dot_general(
        flat_rows, flat_dlogit, (((0,), (0,)), ((), ())), preferred_element_type=jnp.float32
    ).astype(jnp.bfloat16)
    head_group = lax.all_to_all(head_weight, SECTION, split_axis=0, concat_axis=1, tiled=True)
    folded = jnp.einsum(
        "etv,dv->etd",
        lax.all_gather(dlogit, SECTION, axis=2, tiled=True),
        head_group,
        preferred_element_type=jnp.float32,
    )
    grad_normed = sum_at_owner(folded, VOCAB, 1)
    weighted = gains * grad_normed
    inner = lax.psum(jnp.sum(weighted * hidden, axis=-1), SECTION)[..., None]
    grad_hidden = (inverse * weighted - hidden * inverse**3 * inner / D).astype(jnp.bfloat16)
    return (divergence, grad_hidden, grad_head)


def solution(mesh):
    finer = Mesh(
        mesh.devices.reshape(4, 2, 4, 2, 2),
        ("section_0", "section_1", "vocab_0", "vocab_1", "vocab_2"),
    )
    return jax.shard_map(
        body,
        mesh=finer,
        in_specs=(
            P(None, VOCAB, SECTION),
            P(None, SECTION),
            P(None, SECTION_VOCAB),
            P(VOCAB, SECTION),
        ),
        out_specs=(P(), P(None, VOCAB, SECTION), P(None, SECTION_VOCAB)),
        check_vma=False,
    )
```

profile of v0, /device:TPU:0, one launch (start us, length us, event | category | flops | bytes accessed | tf_op | source)
XLA Modules:
  0.0 500.9 jit_solution(9119215491961634991)
XLA Ops:
  7.2 1.0 fusion.8
  8.2 24.6 %psum.14 = f32[3,16]{1,0:T(4,128)S(1)} all-reduce(f32[3,16]{1,0:T(4,128)S(1)} %fusion.8), channel_id=1, replica_groups=mesh['section_0'=4,'section_1'=2,'vocab_0'=4,'vocab_1'=2,'vocab_2'=2] {'..., use_global_device_ids=true, to_apply=%region_1.0 | all-reduce | flops 48 | bytes 384 | tf_op jit(solution)/shard_map/psum | solution.py:65
  32.8 1.6 fusion.10
  34.5 30.6 %all-gather.14.cloned.1.call-done = bf16[3,256,1024]{2,1,0:T(8,128)(2,1)} async-done(((bf16[3,16,1024]{2,1,0:T(8,128)(2,1)}), bf16[3,256,1024]{2,1,0:T(8,128)(2,1)}) %all-gather.14.cloned.1.call-update) | async-done | bytes 1572880 | tf_op jit(solution)/shard_map/all_gather | solution.py:69
  65.2 1.1 copy.25
  66.3 14.6 %all_to_all.43 = f32[16,16,512]{2,0,1:T(8,128)S(1)} all-to-all(f32[16,16,512]{2,0,1:T(8,128)S(1)} %bitcast.292), channel_id=1, replica_groups=mesh['section_0'=4,'section_1'=2,'vocab_0'=4,'vocab_1'=2,'vocab_2'=2] {'..., dimensions={1} | all-to-all | bytes 1048576 | tf_op jit(solution)/shard_map/all_to_all | solution.py:68
  81.3 130.3 %all-gather.16.cloned.1.call-done = bf16[3,256,8192]{2,1,0:T(8,128)(2,1)} async-done(((bf16[3,256,1024]{2,1,0:T(8,128)(2,1)}), bf16[3,256,8192]{2,1,0:T(8,128)(2,1)}) %all-gather.16.cloned.1.call-update) | async-done | bytes 12582928 | tf_op jit(solution)/shard_map/all_gather | solution.py:70
  211.6 11.9 %fusion.70 = (f32[3,256]{1,0:T(4,128)S(1)}, f32[3,256,512]{2,1,0:T(8,128)S(1)}) fusion(bf16[3,256,8192]{2,1,0:T(8,128)(2,1)} %all-gather.16.cloned.1.call-done, bf16[8192,512]{1,0:T(8,128)(2,1)} %param.6), kind=kOutput, calls=%fused_computation.128 | convolution fusion | flops 6442843136 | bytes 22547456 | tf_op jit(solution)/shard_map/dot_general | solution.py:75
  224.2 11.9 %all-gather.5 = f32[4,10,256]{2,1,0:T(8,128)S(1)} all-gather(f32[1,10,256]{2,1,0:T(8,128)S(1)} %maximum_bitcast_fusion), channel_id=2, replica_groups=mesh['section_0'=4,'section_1'=2,'vocab_0'=4,'vocab_1'=2,'vocab_2'=2] {'..., dimensions={0}, use_global_device_ids=true | all-gather | bytes 51200 | tf_op jit(solution)/shard_map/all_gather | solution.py:26
  236.2 5.9 %all-gather.6 = f32[2,10,256]{2,1,0:T(8,128)S(1)} all-gather(f32[1,10,256]{2,1,0:T(8,128)S(1)} %maximum_bitcast_fusion.1), channel_id=3, replica_groups=mesh['section_0'=4,'section_1'=2,'vocab_0'=4,'vocab_1'=2,'vocab_2'=2] {'..., dimensions={0}, use_global_device_ids=true | all-gather | bytes 30720 | tf_op jit(solution)/shard_map/all_gather | solution.py:26
  242.1 12.3 %all-gather.7 = f32[4,10,256]{2,1,0:T(8,128)S(1)} all-gather(f32[1,10,256]{2,1,0:T(8,128)S(1)} %maximum_bitcast_fusion.2), channel_id=4, replica_groups=mesh['section_0'=4,'section_1'=2,'vocab_0'=4,'vocab_1'=2,'vocab_2'=2] {'..., dimensions={0}, use_global_device_ids=true | all-gather | bytes 51200 | tf_op jit(solution)/shard_map/all_gather | solution.py:26
  254.5 4.4 all-gather.8
  259.0 1.8 all-gather.9
  261.0 1.3 multiply_convert_fusion
  262.2 123.0 %all_to_all.44 = bf16[8,1024,512]{2,1,0:T(8,128)(2,1)} all-to-all(bf16[8,1024,512]{2,1,0:T(8,128)(2,1)} %bitcast.291), channel_id=1, replica_groups=mesh['section_0'=4,'section_1'=2,'vocab_0'=4,'vocab_1'=2,'vocab_2'=2] {'..., dimensions={0} | all-to-all | bytes 16777216 | tf_op jit(solution)/shard_map/all_to_all | solution.py:95
  385.3 11.6 %copy.17 = bf16[1024,8,512]{2,1,0:T(8,128)(2,1)} copy(bf16[1024,8,512]{2,0,1:T(8,128)(2,1)} %bitcast.288) | data formatting | bytes 16777216 | tf_op jit(solution)/shard_map/all_to_all | solution.py:95
  396.9 13.5 %reshape.285 = bf16[1024,4096,1,1]{1,0,2,3:T(8,128)(2,1)} reshape(bf16[1024,8,512]{2,1,0:T(8,128)(2,1)} %copy.17) | data formatting | bytes 16777216 | tf_op jit(solution)/shard_map/all_to_all | solution.py:95
  410.4 6.6 %all-gather.18.cloned.1.call-done = bf16[3,256,4096]{2,1,0:T(8,128)(2,1)} async-done(((bf16[3,256,512]{2,1,0:T(8,128)(2,1)}), bf16[3,256,4096]{2,1,0:T(8,128)(2,1)}) %all-gather.18.cloned.1.call-update) | async-done | bytes 6291472 | tf_op jit(solution)/shard_map/all_gather | solution.py:98
  417.0 11.0 %fusion.4 = f32[16,3,16,1024]{3,2,0,1:T(8,128)S(1)} fusion(bf16[3,16,16,4096]{3,2,1,0:T(8,128)(2,1)} %bitcast.295, bf16[1024,4096,1,1]{1,0,2,3:T(8,128)(2,1)} %reshape.285), kind=kOutput, calls=%fused_computation.5 | convolution fusion | flops 6442450944 | bytes 17825792 | tf_op jit(solution)/shard_map/etv,dv->etd/dot_general | solution.py:96
  428.0 1.9 copy.18
  429.9 4.0 all-to-all-start.2
  434.4 13.8 %bitcast_convert_fusion = bf16[8192,512]{1,0:T(8,128)(2,1)} fusion(bf16[3,256,8192]{2,1,0:T(8,128)(2,1)} %all-gather.16.cloned.1.call-done, bf16[3,256,512]{2,1,0:T(8,128)(2,1)} %multiply_convert_fusion), kind=kOutput, calls=%fused_computation | convolution fusion | flops 6446645248 | bytes 21757952 | tf_op jit(solution)/shard_map/dot_general | solution.py:92
  448.2 24.5 %all-to-all-done.2 = f32[16,3,16,1024]{3,2,1,0:T(8,128)S(1)} async-done(((f32[16,3,16,1024]{3,2,1,0:T(8,128)}), f32[16,3,16,1024]{3,2,1,0:T(8,128)S(1)}, u32[]{:S(2)}, u32[]{:S(2)}) %all-to-all-start.2) | async-done | bytes 3145760 | tf_op jit(solution)/shard_map/all_to_all | solution.py:52
  473.1 20.5 %psum.15 = f32[3,16]{1,0:T(4,128)S(1)} all-reduce(f32[3,16]{1,0:T(4,128)S(1)} %fusion.15), channel_id=1, replica_groups=mesh['section_0'=4,'section_1'=2,'vocab_0'=4,'vocab_1'=2,'vocab_2'=2] {'..., use_global_device_ids=true, to_apply=%region_9.10 | all-reduce | flops 48 | bytes 384 | tf_op jit(solution)/shard_map/psum | solution.py:104
  (38 shorter events, 3.1 us)
Async XLA Ops:
  7.2 58.0 %all-gather.14.cloned.1.call-start = ((), (), s32[]{:S(2)}) async-start(), calls=%async_computation.3 | async-start | bytes 1671168 | tf_op jit(solution)/shard_map/all_gather | solution.py:69
  34.5 177.1 %all-gather.16.cloned.1.call-start = ((), (), s32[]{:S(2)}) async-start(), calls=%async_computation.4 | async-start | bytes 14155776 | tf_op jit(solution)/shard_map/all_gather | solution.py:70
  65.2 351.8 %all-gather.18.cloned.1.call-start = ((), (), s32[]{:S(2)}) async-start(), calls=%async_computation.5 | async-start | bytes 7077888 | tf_op jit(solution)/shard_map/all_gather | solution.py:98
  429.9 42.9 %all-to-all-start.2 = ((f32[16,3,16,1024]{3,2,1,0:T(8,128)}), f32[16,3,16,1024]{3,2,1,0:T(8,128)S(1)}, u32[]{:S(2)}, u32[]{:S(2)}) async-start(f32[16,3,16,1024]{3,2,1,0:T(8,128)} %copy.18), calls=%async_computation.2 | async-start | bytes 6291456 | tf_op jit(solution)/shard_map/all_to_all | solution.py:52
  434.4 38.6 %copy-start = (bf16[3,16,1024]{2,1,0:T(8,128)(2,1)S(1)}, bf16[3,16,1024]{2,1,0:T(8,128)(2,1)}, u32[]{:S(2)}) copy-start(bf16[3,16,1024]{2,1,0:T(8,128)(2,1)} %param.4) | copy-start | bytes 294916
  434.4 38.6 %copy-start.1 = (f32[3,1024]{1,0:T(4,128)S(1)}, f32[3,1024]{1,0:T(4,128)}, u32[]{:S(2)}) copy-start(f32[3,1024]{1,0:T(4,128)} %param.5) | copy-start | bytes 36868
Sparse Core Ops, SparseCore 0:
  34.6 30.5 all-gather.13
  67.5 144.0 all-gather.15
  262.4 154.5 all-gather.17
where the time goes:
time: 502 us; the launch traced here: 501 us
  blocking collectives  219 us (44%)
  waiting for transfers between devices  192 us (38%)
  matrix products  36.7 us (7%)
  local copies, waits for them, and re-layouts  28.2 us (6%)
  between operations  13.9 us (3%)
  other arithmetic  6.65 us (1%)
    all_gather x1, waiting for transfers between devices, body(): gathered = lax.all_gather(token_full, SECTION, axis=2, tiled=True)  130 us
    all_to_all x1, blocking collectives, body(): lax.all_to_all(head_weight, SECTION, split_axis=0, concat_axis=1, tiled=T...  123 us
    all_gather x5, blocking collectives, gathered_once(): both, at, found = (lax.all_gather(jnp.concatenate(lines), axis), 0, {})  36.4 us
    all_gather x1, waiting for transfers between devices, body(): token_full = lax.all_gather(normed, VOCAB, axis=1, tiled=True)  30.6 us
    all_to_all x2, local copies, waits for them, and re-layouts, body(): lax.all_to_all(head_weight, SECTION, split_axis=0, concat_axis=1, tiled=T...  25.1 us
    psum x1, blocking collectives, body(): squares = lax.psum(jnp.sum(hidden * hidden, axis=-1), SECTION)  24.6 us
    all_to_all x1, waiting for transfers between devices, sum_at_owner(): lax.all_to_all(cut_along(value, dim, length), axis, 0, 0, tiled=True)  24.5 us
    psum x1, blocking collectives, body(): inner = lax.psum(jnp.sum(weighted * hidden, axis=-1), SECTION)[..., None]  20.5 us
  transfers between devices with their start and end apart: 4, of which 4 were waited for; matrix products, arithmetic and copies ran while one was open for 8% of the time, Pallas kernels for 0%

commit v1 on v0

v1 whole, which is shorter than its diff:
```python
import functools

import jax
import jax.numpy as jnp
from jax import lax
from jax.experimental import pallas as pl
from jax.experimental.pallas import tpu as pltpu
from jax.sharding import PartitionSpec as P

MESH = pl.DeviceIdType.MESH
EXITS = 3
ROWS = 16
TOKENS = 256
epsilon = 1e-05
loss_scale = 1024.0
AXES = ("x", "y", "z")
ORDER = (("y", "z", "x"), ("z", "x", "y"), ("x", "y", "z"))
bf16 = jnp.bfloat16
f32 = jnp.float32


def chip(x, y, z, c):
    return (y * 2 + lax.div(x, 2), z * 4 + lax.rem(x, 2) * 2 + c)


def place():
    s, v = lax.axis_index("section"), lax.axis_index("vocab")
    x = lax.rem(s, 2) * 2 + lax.rem(lax.div(v, 2), 2)
    return s, v, dict(x=x, y=lax.div(s, 2), z=lax.div(v, 4)), lax.rem(v, 2)


def turned(k, by):
    return lax.rem(k + by, 4)


class Copies:
    def __init__(self, send_sem, recv_sem):
        self.send_sem, self.recv_sem, self.made = send_sem, recv_sem, []

    def start(self, src, dst, device):
        n = len(self.made)
        copy = pltpu.make_async_remote_copy(
            src_ref=src,
            dst_ref=dst,
            send_sem=self.send_sem.at[n],
            recv_sem=self.recv_sem.at[n],
            device_id=device,
            device_id_type=MESH,
        )
        copy.start()
        self.made.append(copy)
        return copy

    def finish(self):
        for copy in self.made:
            copy.wait_send()


def neighbour(pos, c, axis, by):
    there = dict(pos)
    there[axis] = turned(pos[axis], by)
    return chip(**there, c=c)


def greet(devices):
    barrier = pltpu.get_barrier_semaphore()
    for device in devices:
        pl.semaphore_signal(barrier, inc=1, device_id=device, device_id_type=MESH)
    return lambda: pl.semaphore_wait(barrier, len(devices))


def section_peers(s, v):
    return [(lax.rem(s + k, 8), v) for k in range(1, 8)]


def vocab_peers(s, v):
    return [(s, lax.rem(v + k, 16)) for k in range(1, 16)]


def to_all(copies, slots, me, peers):
    sent = [copies.start(slots.at[me], slots.at[me], peer) for peer in peers]
    for copy in sent:
        copy.wait_recv()


def by_lane(columns, rows):
    lane = lax.broadcasted_iota(jnp.int32, (rows, 128), 1)
    tile = jnp.zeros((rows, 128), f32)
    for k, column in enumerate(columns):
        tile = jnp.where(lane == k, column, tile)
    return tile


def column_of(tile, k):
    lane = lax.broadcasted_iota(jnp.int32, tile.shape, 1)
    return jnp.sum(jnp.where(lane == k, tile, 0.0), axis=1, keepdims=True)


def slots_sum(slots, count):
    total = slots[0]
    for k in range(1, count):
        total = total + slots[k]
    return total


def merged(slots, count):
    top = slots[0]
    for k in range(1, count):
        top = jnp.maximum(top, slots[k])
    exps = jnp.zeros(top.shape, f32)
    sums = jnp.zeros(top.shape, f32)
    for k in range(count):
        part = slots[k]
        exps = exps + jnp.exp(part - top)
        sums = sums + part
    row = lax.broadcasted_iota(jnp.int32, top.shape, 0)
    return jnp.where(row < EXITS, top + jnp.log(exps), sums)


def forward_kernel(
    hidden, gain, teacher, head_hbm, full_hbm, dlogit, divergence, inverse,
    full, head, logits, target, square_slots, vocab_slots, section_slots,
    send_sem, recv_sem, head_sem, full_sem,
):
    width, cols = hidden.shape[2], head.shape[1]
    s, v, pos, c = place()
    x, y, z = pos["x"], pos["y"], pos["z"]
    xh, xl = lax.div(x, 2), lax.rem(x, 2)
    copies = Copies(send_sem, recv_sem)
    head_copy = pltpu.make_async_copy(head_hbm, head, head_sem)
    head_copy.start()
    beyond = neighbour(pos, c, "x", 3 + 2 * xl)
    ready = greet(vocab_peers(s, v) + section_peers(s, v) + [beyond])

    squares = [
        jnp.sum(jnp.square(hidden[e].astype(f32)), axis=1, keepdims=True) for e in range(EXITS)
    ]
    square_slots[s] = by_lane(squares, ROWS)
    ready()
    to_all(copies, square_slots, s, section_peers(s, v))
    inverse[...] = lax.rsqrt(slots_sum(square_slots, 8) / (8 * width) + epsilon)
    for e in range(EXITS):
        scale = column_of(inverse[...], e)
        full[y, xh, e, z, xl, c] = (hidden[e].astype(f32) * scale * gain[e]).astype(bf16)

    half = width // 2

    def region(e, over, whole, part):
        at = {**pos, **over}
        every = slice(None)
        yi, zi = (every if a in whole else at[a] for a in ("y", "z"))
        xhi = every if "x" in whole else lax.div(at["x"], 2)
        xli = every if "x" in whole else lax.rem(at["x"], 2)
        columns = every if part is None else slice(part * half, (part + 1) * half)
        return full.at[yi, xhi, e, zi, xli, c, :, columns]

    partner = chip(**pos, c=1 - c)
    swaps = []

    def swap(ref):
        swaps.append(copies.start(ref, ref, partner))

    for turn in range(3):
        last = turn == 2
        pieces = []
        for e in range(EXITS):
            axis, whole = ORDER[e][turn], ORDER[e][:turn]
            after, before = (neighbour(pos, c, axis, by) for by in (1, 3))
            low, high = region(e, {}, whole, 0), region(e, {}, whole, 1)
            up_low = copies.start(low, low, after)
            down_high = copies.start(high, high, before)
            up_high = copies.start(high, high, after)
            down_low = copies.start(low, low, before)
            pieces.append((up_low, down_high, up_high, down_low))
        if last:
            for e in range(EXITS):
                swap(region(e, {}, ORDER[e][:2], None))
        relays = []
        for e in range(EXITS):
            axis, whole = ORDER[e][turn], ORDER[e][:turn]
            after, before = (neighbour(pos, c, axis, by) for by in (1, 3))
            up_low, down_high, _, _ = pieces[e]
            up_low.wait_recv()
            block = region(e, {axis: turned(pos[axis], 3)}, whole, 0)
            up = copies.start(block, block, after)
            if last:
                swap(block)
            down_high.wait_recv()
            block = region(e, {axis: turned(pos[axis], 1)}, whole, 1)
            down = copies.start(block, block, before)
            if last:
                swap(block)
            relays.append((up, down))
        for e in range(EXITS):
            axis, whole = ORDER[e][turn], ORDER[e][:turn]
            pieces[e][2].wait_recv()
            if last:
                swap(region(e, {axis: turned(pos[axis], 3)}, whole, 1))
            pieces[e][3].wait_recv()
            if last:
                swap(region(e, {axis: turned(pos[axis], 1)}, whole, 0))
        if last:
            lent = [
                copies.start(
                    teacher.at[:, pl.ds(pl.multiple_of(peer[1] * cols, 128), cols)],
                    target.at[v],
                    peer,
                )
                for peer in vocab_peers(s, v)
            ]
            target[v] = teacher[:, pl.ds(pl.multiple_of(v * cols, 128), cols)]
        for e in range(EXITS):
            axis, whole = ORDER[e][turn], ORDER[e][:turn]
            for k in range(2):
                relays[e][k].wait_recv()
                if last:
                    swap(region(e, {axis: turned(pos[axis], 2)}, whole, k))
    for copy in swaps:
        copy.wait_recv()
    full_copy = pltpu.make_async_copy(full, full_hbm, full_sem)
    full_copy.start()
    head_copy.wait()

    logits[...] = jnp.zeros(logits.shape, f32)

    def multiply(k, _):
        rows = full[lax.div(k, 2), lax.rem(k, 2)].reshape(EXITS * TOKENS, width)
        columns = head[pl.ds(pl.multiple_of(k * width, 128), width), :]
        logits[...] += jnp.dot(rows, columns, preferred_element_type=f32)
        return 0

    lax.fori_loop(0, 8, multiply, 0)
    for copy in lent:
        copy.wait_recv()

    columns = []
    for e in range(EXITS):
        block = logits[e * TOKENS : (e + 1) * TOKENS, :]
        top = jnp.max(block, axis=1, keepdims=True)
        columns.append(top + jnp.log(jnp.sum(jnp.exp(block - top), axis=1, keepdims=True)))
    stored = target[...].reshape(TOKENS, cols)
    weight = jnp.exp(stored)
    for e in range(EXITS):
        block = logits[e * TOKENS : (e + 1) * TOKENS, :]
        columns.append(jnp.sum(weight * (stored - block), axis=1, keepdims=True))
    columns.append(jnp.sum(weight, axis=1, keepdims=True))
    vocab_slots[v] = jnp.transpose(by_lane(columns, TOKENS))[:8]
    to_all(copies, vocab_slots, v, vocab_peers(s, v))
    section_slots[s] = merged(vocab_slots, 16)
    to_all(copies, section_slots, s, section_peers(s, v))
    rows = merged(section_slots, 8)
    terms = rows[EXITS : 2 * EXITS] + rows[:EXITS] * rows[2 * EXITS : 2 * EXITS + 1]
    mean = jnp.sum(terms, axis=1, keepdims=True) / TOKENS
    divergence[...] = jnp.broadcast_to(mean, (EXITS, 128))
    turned_rows = jnp.transpose(jnp.concatenate([rows, jnp.zeros((120, TOKENS), f32)], axis=0))
    for e in range(EXITS):
        block = logits[e * TOKENS : (e + 1) * TOKENS, :]
        log_total = turned_rows[:, e : e + 1]
        grad = (jnp.exp(block - log_total) - weight) * (loss_scale / TOKENS)
        dlogit[e * TOKENS : (e + 1) * TOKENS, :] = grad.astype(bf16)
    copies.finish()
    full_copy.wait()


def backward_kernel(
    dlogit, hidden, gain, inverse, head_hbm, grad_hidden,
    head, partial, swapped, held, first, second, third, summed, inner_slots,
    send_sem, recv_sem, swap_send, swap_recv, head_sem,
):
    width = hidden.shape[2]
    s, v, pos, c = place()
    x, y, z = pos["x"], pos["y"], pos["z"]
    copies = Copies(send_sem, recv_sem)

    def head_copy(k):
        rows = pl.ds(pl.multiple_of(k * width, 128), width)
        return pltpu.make_async_copy(head_hbm.at[rows, :], head.at[rows, :], head_sem.at[k])

    for k in range(8):
        head_copy(k).start()
    partner = chip(**pos, c=1 - c)
    near = [neighbour(pos, c, axis, by) for axis in ("x", "z") for by in (1, 3)]
    ready = greet([partner] + section_peers(s, v) + near)
    ready()

    def swap(k):
        yk, xk = lax.div(k, 2), lax.rem(k, 2)
        return pltpu.make_async_remote_copy(
            src_ref=partial.at[yk, xk, :, :, :, 1 - c],
            dst_ref=swapped.at[yk, xk],
            send_sem=swap_send.at[k],
            recv_sem=swap_recv.at[k],
            device_id=partner,
            device_id_type=MESH,
        )

    def multiply(k, _):
        head_copy(k).wait()
        rows = head[pl.ds(pl.multiple_of(k * width, 128), width), :]
        part = lax.dot_general(
            dlogit[...], rows, (((1,), (1,)), ((), ())), preferred_element_type=f32
        )
        partial[lax.div(k, 2), lax.rem(k, 2)] = part.astype(bf16).reshape(EXITS, 4, 2, 2, ROWS, width)
        swap(k).start()
        return 0

    lax.fori_loop(0, 8, multiply, 0)

    def add_swapped(k, _):
        yk, xk = lax.div(k, 2), lax.rem(k, 2)
        swap(k).wait_recv()
        for e in range(EXITS):
            for low in range(2):
                mine = partial[yk, xk, e, :, low, c].astype(f32)
                theirs = swapped[yk, xk, e, :, low].astype(f32)
                held[e, xk * 2 + low, yk] = (mine + theirs).astype(bf16)
        return 0

    lax.fori_loop(0, 8, add_swapped, 0)

    half = width // 2

    def columns_of(part):
        return slice(part * half, (part + 1) * half)

    def block(e, axis, at, rest, part):
        index = [
            slice(None) if a in rest else (at if a == axis else pos[a]) for a in AXES
        ]
        return held.at[(e, *index, slice(None), columns_of(part))]

    def add(e, axis, at, rest, part, arrived):
        def step(n, _):
            digits, index = n, {**pos, axis: at}
            found = []
            for a in reversed(rest):
                found.insert(0, lax.rem(digits, 4))
                index[a] = found[0]
                digits = lax.div(digits, 4)
            ref = held.at[e, index["x"], index["y"], index["z"], :, columns_of(part)]
            total = ref[...].astype(f32)
            for slot in arrived:
                total = total + slot[tuple(found)].astype(f32)
            ref[...] = total.astype(bf16)
            return 0

        lax.fori_loop(0, 4 ** len(rest), step, 0)

    for turn, slots in enumerate((first, second, third)):
        went = []
        plan = []
        for e in range(EXITS):
            axis = ORDER[e][2 - turn]
            rest = tuple(a for a in AXES if a in ORDER[e][: 2 - turn])
            here = pos[axis]
            after, before = (neighbour(pos, c, axis, by) for by in (1, 3))
            plan.append((axis, rest, here, after, before))
            up, down, far = turned(here, 1), turned(here, 3), turned(here, 2)
            went.append(
                [
                    copies.start(block(e, axis, far, rest, 0), slots.at[e, 0], after),
                    copies.start(block(e, axis, far, rest, 1), slots.at[e, 1], before),
                    copies.start(block(e, axis, up, rest, 1), slots.at[e, 3], after),
                    copies.start(block(e, axis, down, rest, 0), slots.at[e, 4], before),
                ]
            )
        for e in range(EXITS):
            axis, rest, here, after, before = plan[e]
            up, down = turned(here, 1), turned(here, 3)
            went[e][0].wait_recv()
            add(e, axis, up, rest, 0, [slots.at[e, 0]])
            went[e].append(copies.start(block(e, axis, up, rest, 0), slots.at[e, 2], after))
            went[e][1].wait_recv()
            add(e, axis, down, rest, 1, [slots.at[e, 1]])
            went[e].append(copies.start(block(e, axis, down, rest, 1), slots.at[e, 5], before))
        for e in range(EXITS):
            axis, rest, here, after, before = plan[e]
            for k in range(2, 6):
                went[e][k].wait_recv()
            if turn < 2:
                add(e, axis, here, rest, 0, [slots.at[e, 2], slots.at[e, 4]])
                add(e, axis, here, rest, 1, [slots.at[e, 3], slots.at[e, 5]])
            else:
                for part in range(2):
                    own = held[e, x, y, z, :, columns_of(part)].astype(f32)
                    near_two = slots[e, 2 + part].astype(f32) + slots[e, 4 + part].astype(f32)
                    summed[e, :, columns_of(part)] = own + near_two

    sums = []
    for e in range(EXITS):
        weighted = gain[e] * summed[e]
        summed[e] = weighted
        sums.append(jnp.sum(weighted * hidden[e].astype(f32), axis=1, keepdims=True))
    inner_slots[s] = by_lane(sums, ROWS)
    to_all(copies, inner_slots, s, section_peers(s, v))
    inner = slots_sum(inner_slots, 8)
    cube = inverse[...] * inverse[...] * inverse[...] * inner / (8 * width)
    for e in range(EXITS):
        scale = column_of(inverse[...], e)
        back = scale * summed[e] - hidden[e].astype(f32) * column_of(cube, e)
        grad_hidden[e] = back.astype(bf16)
    copies.finish()
    for k in range(8):
        swap(k).wait_send()


def body(exit_hidden, norm_gain, head_weight, teacher):
    width, cols = exit_hidden.shape[2], head_weight.shape[1]
    gain = norm_gain[:, None, :]
    vmem = pl.BlockSpec(memory_space=pltpu.VMEM)
    hbm = pl.BlockSpec(memory_space=pl.ANY)
    tile = (4, 2, EXITS, 4, 2, 2, ROWS, width)
    dma = pltpu.SemaphoreType.DMA
    full, dlogit, divergence, inverse = pl.pallas_call(
        forward_kernel,
        out_shape=(
            jax.ShapeDtypeStruct(tile, bf16),
            jax.ShapeDtypeStruct((EXITS * TOKENS, cols), bf16),
            jax.ShapeDtypeStruct((EXITS, 128), f32),
            jax.ShapeDtypeStruct((ROWS, 128), f32),
        ),
        in_specs=[vmem, vmem, vmem, hbm],
        out_specs=(hbm, vmem, vmem, vmem),
        scratch_shapes=[
            pltpu.VMEM(tile, bf16),
            pltpu.VMEM((8 * width, cols), bf16),
            pltpu.VMEM((EXITS * TOKENS, cols), f32),
            pltpu.VMEM((16, ROWS, cols), f32),
            pltpu.VMEM((8, ROWS, 128), f32),
            pltpu.VMEM((16, 8, TOKENS), f32),
            pltpu.VMEM((8, 8, TOKENS), f32),
            dma((119,)),
            dma((119,)),
            dma,
            dma,
        ],
        compiler_params=pltpu.CompilerParams(
            collective_id=0, has_side_effects=True, vmem_limit_bytes=48 * 2**20
        ),
        name="forward",
    )(exit_hidden, gain, teacher, head_weight)
    grad_head = lax.dot_general(
        full.reshape(8, EXITS * TOKENS, width),
        dlogit,
        (((1,), (0,)), ((), ())),
        preferred_element_type=f32,
    ).astype(bf16)
    grad_hidden = pl.pallas_call(
        backward_kernel,
        out_shape=jax.ShapeDtypeStruct(exit_hidden.shape, bf16),
        in_specs=[vmem, vmem, vmem, vmem, hbm],
        out_specs=vmem,
        scratch_shapes=[
            pltpu.VMEM((8 * width, cols), bf16),
            pltpu.VMEM(tile, bf16),
            pltpu.VMEM((4, 2, EXITS, 4, 2, ROWS, width), bf16),
            pltpu.VMEM((EXITS, 4, 4, 4, ROWS, width), bf16),
            pltpu.VMEM((EXITS, 6, 4, 4, ROWS, width // 2), bf16),
            pltpu.VMEM((EXITS, 6, 4, ROWS, width // 2), bf16),
            pltpu.VMEM((EXITS, 6, ROWS, width // 2), bf16),
            pltpu.VMEM((EXITS, ROWS, width), f32),
            pltpu.VMEM((8, ROWS, 128), f32),
            dma((61,)),
            dma((61,)),
            dma((8,)),
            dma((8,)),
            dma((8,)),
        ],
        compiler_params=pltpu.CompilerParams(
            collective_id=1, has_side_effects=True, vmem_limit_bytes=56 * 2**20
        ),
        name="backward",
    )(dlogit, exit_hidden, gain, inverse, head_weight)
    return divergence[:, 0], grad_hidden, grad_head.reshape(8 * width, cols)


def solution(mesh):
    return jax.shard_map(
        body,
        mesh=mesh,
        in_specs=(
            P(None, "vocab", "section"),
            P(None, "section"),
            P(None, ("section", "vocab")),
            P("vocab", "section"),
        ),
        out_specs=(P(), P(None, "vocab", "section"), P(None, ("section", "vocab"))),
        check_vma=False,
    )
```

time: 502 us -> 147 us (0.29)
  blocking collectives: 219 us -> 0 us
  waiting for transfers between devices: 192 us -> 0 us
  Pallas kernels: 0 us -> 127 us
  local copies, waits for them, and re-layouts: 28.2 us -> 5.44 us
  matrix products: 36.7 us -> 14.1 us
  between operations: 13.9 us -> 0.68 us
  other arithmetic: 6.65 us -> 0 us
    all_gather x3 -> x0, waiting for transfers between devices: 168 us -> none  [the longest x1 130 us: body(): gathered = lax.all_gather(token_full, SECTION, axis=2, tiled=True)]
    all_to_all x2 -> x0, blocking collectives: 138 us -> none  [the longest x1 123 us: body(): lax.all_to_all(head_weight, SECTION, split_axis=0, concat_axis=1, tiled=T...]
    pallas_call x0 -> x2, Pallas kernels: none -> 127 us  [the longest x1 68.5 us: body(): pl.pallas_call(forward_kernel, out_shape=(jax.ShapeDtypeStruct(tile, bf16...]
    psum x2 -> x0, blocking collectives: 45.1 us -> none  [the longest x1 24.6 us: body(): squares = lax.psum(jnp.sum(hidden * hidden, axis=-1), SECTION)]
    all_gather x5 -> x0, blocking collectives: 36.4 us -> none  [gathered_once(): both, at, found = (lax.all_gather(jnp.concatenate(lines), axis), 0, {})]
    all_to_all x3 -> x0, local copies, waits for them, and re-layouts: 26.2 us -> none  [the longest x2 25.1 us: body(): lax.all_to_all(head_weight, SECTION, split_axis=0, concat_axis=1, tiled=T...]
    all_to_all x1 -> x0, waiting for transfers between devices: 24.5 us -> none  [sum_at_owner(): lax.all_to_all(cut_along(value, dim, length), axis, 0, 0, tiled=True)]
    dot_general x3 -> x1, matrix products: 36.7 us -> 14.1 us  [body(): lax.dot_general(full.reshape(8, EXITS * TOKENS, width), dlogit, (((1,), (...]
  transfers between devices with their start and end apart: 4 -> 0, of which waited for: 4 -> 0; matrix products, arithmetic and copies ran while one was open for 8% -> 0% of each run, Pallas kernels for 0% -> 0%
where the time goes in v1:
time: 147 us
  Pallas kernels  127 us (86%)
  matrix products  14.1 us (10%)
  local copies, waits for them, and re-layouts  5.44 us (4%)
    pallas_call x1, Pallas kernels, body(): pl.pallas_call(forward_kernel, out_shape=(jax.ShapeDtypeStruct(tile, bf16...  68.5 us
    pallas_call x1, Pallas kernels, body(): pl.pallas_call(backward_kernel, out_shape=jax.ShapeDtypeStruct(exit_hidde...  58.1 us
    dot_general x1, matrix products, body(): lax.dot_general(full.reshape(8, EXITS * TOKENS, width), dlogit, (((1,), (...  14.1 us
    unnamed x13, local copies, waits for them, and re-layouts  4.09 us

profile of v1, /device:TPU:0, one launch (start us, length us, event | category | flops | bytes accessed | tf_op | source)
XLA Modules:
  0.0 146.8 jit_solution(16354226936124046892)
XLA Ops:
  0.6 0.7 broadcast_in_dim.3.gain
  1.4 0.0 copy-start.1
  1.4 1.0 copy-done.1
  2.4 0.0 copy-start.2
  2.4 0.9 copy-done.2
  3.3 0.0 copy-start.3
  3.3 68.5 %forward.1 = (bf16[4,2,3,4,2,2,16,1024]{7,6,5,4,3,2,1,0:T(8,128)(2,1)}, bf16[768,512]{1,0:T(8,128)(2,1)S(1)}, f32[3,128]{1,0:T(4,128)S(1)}, f32[16,128]{1,0:T(8,128)S(1)}) custom-call(bf16[3,16,1024]{2,1,0:T(8,128)(2,1)S(1)} %copy-done.2, f32[3,1,1024]{2,1,0:T(1,128)S(1)} %broadcast_in_dim.3.gain, f32[16,8192]{1,0:T(8,128)S(1)} %copy-done.1, ...), custom_call_target="tpu_custom_call" | custom-call | tf_op jit(solution)/shard_map/forward/pallas_call | solution.py:414
  71.8 0.0 copy-start
  71.8 0.9 copy-done
  72.8 0.0 copy-start.4
  72.8 0.6 copy-done.4
  73.4 0.6 slice_reduce_fusion
  74.0 0.0 copy-done.3
  74.0 58.1 %backward.1 = bf16[3,16,1024]{2,1,0:T(8,128)(2,1)} custom-call(bf16[768,512]{1,0:T(8,128)(2,1)} %copy-done, bf16[3,16,1024]{2,1,0:T(8,128)(2,1)} %hidden.3, f32[3,1,1024]{2,1,0:T(1,128)} %copy-done.3, f32[16,128]{1,0:T(8,128)} %copy-done.4, bf16[8192,512]{1,0:T(8,128)(2,1)} %head_hbm.3), custom_call_target="tpu_custom_call" | custom-call | tf_op jit(solution)/shard_map/backward/pallas_call | solution.py:448
  132.1 0.0 copy-start.5
  132.1 14.1 %convolution_convert_fusion = bf16[8,1024,512]{2,1,0:T(8,128)(2,1)} fusion(bf16[8,768,1024]{2,1,0:T(8,128)(2,1)} %bitcast.6, bf16[768,512]{1,0:T(8,128)(2,1)} %copy-done), kind=kOutput, calls=%fused_computation | convolution fusion | flops 6446645248 | bytes 21757952 | tf_op jit(solution)/shard_map/dot_general | solution.py:442
  146.1 0.0 copy-done.5
  146.1 0.6 copy.11
Async XLA Ops:
  1.4 1.0 copy-start.1
  2.4 0.9 copy-start.2
  3.3 70.7 %copy-start.3 = (f32[3,1,1024]{2,1,0:T(1,128)}, f32[3,1,1024]{2,1,0:T(1,128)S(1)}, u32[]{:S(2)}) copy-start(f32[3,1,1024]{2,1,0:T(1,128)S(1)} %broadcast_in_dim.3.gain) | copy-start | bytes 36868
  71.8 0.9 copy-start
  72.8 0.6 copy-start.4
  132.1 14.1 %copy-start.5 = (bf16[3,16,1024]{2,1,0:T(8,128)(2,1)S(1)}, bf16[3,16,1024]{2,1,0:T(8,128)(2,1)}, u32[]{:S(2)}) copy-start(bf16[3,16,1024]{2,1,0:T(8,128)(2,1)} %backward.1) | copy-start | bytes 294916

commit v2 on v1

v2 whole, which is shorter than its diff:
```python
import functools

import jax
import jax.numpy as jnp
from jax import lax
from jax.experimental import pallas as pl
from jax.experimental.pallas import tpu as pltpu
from jax.sharding import PartitionSpec as P

MESH = pl.DeviceIdType.MESH
EXITS = 3
ROWS = 16
TOKENS = 256
epsilon = 1e-05
loss_scale = 1024.0
AXES = ("x", "y", "z")
ORDER = (("y", "z", "x"), ("z", "x", "y"), ("x", "y", "z"))
bf16 = jnp.bfloat16
f32 = jnp.float32


def chip(x, y, z, c):
    return (y * 2 + lax.div(x, 2), z * 4 + lax.rem(x, 2) * 2 + c)


def place():
    s, v = lax.axis_index("section"), lax.axis_index("vocab")
    x = lax.rem(s, 2) * 2 + lax.rem(lax.div(v, 2), 2)
    return s, v, dict(x=x, y=lax.div(s, 2), z=lax.div(v, 4)), lax.rem(v, 2)


def turned(k, by):
    return lax.rem(k + by, 4)


class Copies:
    def __init__(self, send_sem, recv_sem):
        self.send_sem, self.recv_sem, self.made = send_sem, recv_sem, []

    def start(self, src, dst, device):
        n = len(self.made)
        copy = pltpu.make_async_remote_copy(
            src_ref=src,
            dst_ref=dst,
            send_sem=self.send_sem.at[n],
            recv_sem=self.recv_sem.at[n],
            device_id=device,
            device_id_type=MESH,
        )
        copy.start()
        self.made.append(copy)
        return copy

    def finish(self):
        for copy in self.made:
            copy.wait_send()


def neighbour(pos, c, axis, by):
    there = dict(pos)
    there[axis] = turned(pos[axis], by)
    return chip(**there, c=c)


def greet(devices):
    barrier = pltpu.get_barrier_semaphore()
    for device in devices:
        pl.semaphore_signal(barrier, inc=1, device_id=device, device_id_type=MESH)
    return lambda: pl.semaphore_wait(barrier, len(devices))


def section_peers(s, v):
    return [(lax.rem(s + k, 8), v) for k in range(1, 8)]


def vocab_peers(s, v):
    return [(s, lax.rem(v + k, 16)) for k in range(1, 16)]


DIMS = (("y", 4), ("xh", 2), ("z", 4), ("xl", 2))


def split_x(pos):
    return {
        "y": pos["y"],
        "xh": lax.div(pos["x"], 2),
        "z": pos["z"],
        "xl": lax.rem(pos["x"], 2),
    }


def whole_dims(whole):
    return [(d, n) for d, n in DIMS if d[0] in whole]


def to_all(copies, slots, me, peers):
    sent = [copies.start(slots.at[me], slots.at[me], peer) for peer in peers]
    for copy in sent:
        copy.wait_recv()


def by_lane(columns, rows):
    lane = lax.broadcasted_iota(jnp.int32, (rows, 128), 1)
    tile = jnp.zeros((rows, 128), f32)
    for k, column in enumerate(columns):
        tile = jnp.where(lane == k, column, tile)
    return tile


def column_of(tile, k):
    lane = lax.broadcasted_iota(jnp.int32, tile.shape, 1)
    return jnp.sum(jnp.where(lane == k, tile, 0.0), axis=1, keepdims=True)


def slots_sum(slots, count):
    total = slots[0]
    for k in range(1, count):
        total = total + slots[k]
    return total


def merged(slots, count):
    top = slots[0]
    for k in range(1, count):
        top = jnp.maximum(top, slots[k])
    exps = jnp.zeros(top.shape, f32)
    sums = jnp.zeros(top.shape, f32)
    for k in range(count):
        part = slots[k]
        exps = exps + jnp.exp(part - top)
        sums = sums + part
    row = lax.broadcasted_iota(jnp.int32, top.shape, 0)
    return jnp.where(row < EXITS, top + jnp.log(exps), sums)


def kernel(
    hidden_hbm, gain_hbm, teacher_hbm, head_hbm, divergence, grad_hidden, grad_head,
    hidden, gain, teacher, full, head, logits, target, dlogit, inverse, summed, partial, swapped,
    first_0, first_1, first_2, second_0, second_1, second_2, third,
    square_slots, vocab_slots, section_slots, inner_slots,
    send_sem, recv_sem, swap_send, swap_recv, local_sem,
):
    width, cols = hidden.shape[2], head.shape[1]
    half = width // 2
    s, v, pos, c = place()
    x, y, z = pos["x"], pos["y"], pos["z"]
    xh, xl = lax.div(x, 2), lax.rem(x, 2)
    partner = chip(**pos, c=1 - c)
    copies = Copies(send_sem, recv_sem)
    near = [neighbour(pos, c, "x", by) for by in (1, 3)]
    near += [neighbour(pos, c, "z", by) for by in (1, 2, 3)]
    ready = greet([partner] + section_peers(s, v) + near)
    loads = [
        pltpu.make_async_copy(src, dst, local_sem.at[k])
        for k, (src, dst) in enumerate(
            ((hidden_hbm, hidden), (gain_hbm, gain), (head_hbm, head), (teacher_hbm, teacher))
        )
    ]
    for load in loads:
        load.start()
    loads[0].wait()
    squares = [
        jnp.sum(jnp.square(hidden[e].astype(f32)), axis=1, keepdims=True) for e in range(EXITS)
    ]
    square_slots[s] = by_lane(squares, ROWS)
    loads[1].wait()
    ready()
    to_all(copies, square_slots, s, section_peers(s, v))
    inverse[...] = lax.rsqrt(slots_sum(square_slots, 8) / (8 * width) + epsilon)
    for e in range(EXITS):
        scale = column_of(inverse[...], e)
        normed = hidden[e].astype(f32) * scale * gain[e : e + 1, :]
        full[y, xh, e, z, xl, c] = normed.astype(bf16)

    def columns_of(part):
        return slice(None) if part is None else slice(part * half, (part + 1) * half)

    def region(ref, e, over, whole, part):
        at = split_x({**pos, **over})
        for d, _ in whole_dims(whole):
            at[d] = slice(None)
        return ref.at[at["y"], at["xh"], e, at["z"], at["xl"], c, :, columns_of(part)]

    def around(axis):
        return [neighbour(pos, c, axis, by) for by in (1, 2, 3)]

    swaps = []

    def swap(ref):
        swaps.append(copies.start(ref, ref, partner))

    sent = []
    for e in range(EXITS):
        mine = region(full, e, {}, (), None)
        sent += [copies.start(mine, mine, there) for there in around(ORDER[e][0])]
    for copy in sent:
        copy.wait_recv()
    for turn in (1, 2):
        last = turn == 2
        pieces = []
        for e in range(EXITS):
            axis, whole = ORDER[e][turn], ORDER[e][:turn]
            after, _, before = around(axis)
            low, high = region(full, e, {}, whole, 0), region(full, e, {}, whole, 1)
            up_low = copies.start(low, low, after)
            down_high = copies.start(high, high, before)
            up_high = copies.start(high, high, after)
            down_low = copies.start(low, low, before)
            pieces.append((up_low, down_high, up_high, down_low))
        if last:
            for e in range(EXITS):
                swap(region(full, e, {}, ORDER[e][:2], None))
        relays = []
        for e in range(EXITS):
            axis, whole = ORDER[e][turn], ORDER[e][:turn]
            after, _, before = around(axis)
            up_low, down_high, _, _ = pieces[e]
            up_low.wait_recv()
            block = region(full, e, {axis: turned(pos[axis], 3)}, whole, 0)
            up = copies.start(block, block, after)
            if last:
                swap(block)
            down_high.wait_recv()
            block = region(full, e, {axis: turned(pos[axis], 1)}, whole, 1)
            down = copies.start(block, block, before)
            if last:
                swap(block)
            relays.append((up, down))
        for e in range(EXITS):
            axis, whole = ORDER[e][turn], ORDER[e][:turn]
            pieces[e][2].wait_recv()
            if last:
                swap(region(full, e, {axis: turned(pos[axis], 3)}, whole, 1))
            pieces[e][3].wait_recv()
            if last:
                swap(region(full, e, {axis: turned(pos[axis], 1)}, whole, 0))
        if last:
            loads[3].wait()
            lent = [
                copies.start(
                    teacher.at[:, pl.ds(pl.multiple_of(peer[1] * cols, 128), cols)],
                    target.at[v],
                    peer,
                )
                for peer in vocab_peers(s, v)
            ]
            target[v] = teacher[:, pl.ds(pl.multiple_of(v * cols, 128), cols)]
        for e in range(EXITS):
            axis, whole = ORDER[e][turn], ORDER[e][:turn]
            for k in range(2):
                relays[e][k].wait_recv()
                if last:
                    swap(region(full, e, {axis: turned(pos[axis], 2)}, whole, k))
    for copy in swaps:
        copy.wait_recv()
    loads[2].wait()

    logits[...] = jnp.zeros(logits.shape, f32)

    def rows_of(k):
        return full[lax.div(k, 2), lax.rem(k, 2)].reshape(EXITS * TOKENS, width)

    def head_rows(k):
        return pl.ds(pl.multiple_of(k * width, 128), width)

    def multiply(k, _):
        logits[...] += jnp.dot(rows_of(k), head[head_rows(k), :], preferred_element_type=f32)
        return 0

    lax.fori_loop(0, 8, multiply, 0)
    for copy in lent:
        copy.wait_recv()

    columns = []
    for e in range(EXITS):
        block = logits[e * TOKENS : (e + 1) * TOKENS, :]
        top = jnp.max(block, axis=1, keepdims=True)
        columns.append(top + jnp.log(jnp.sum(jnp.exp(block - top), axis=1, keepdims=True)))
    stored = target[...].reshape(TOKENS, cols)
    weight = jnp.exp(stored)
    for e in range(EXITS):
        block = logits[e * TOKENS : (e + 1) * TOKENS, :]
        columns.append(jnp.sum(weight * (stored - block), axis=1, keepdims=True))
    columns.append(jnp.sum(weight, axis=1, keepdims=True))
    vocab_slots[v] = jnp.transpose(by_lane(columns, TOKENS))[:8]
    to_all(copies, vocab_slots, v, vocab_peers(s, v))
    section_slots[s] = merged(vocab_slots, 16)
    to_all(copies, section_slots, s, section_peers(s, v))
    rows = merged(section_slots, 8)
    turned_rows = jnp.transpose(jnp.concatenate([rows, jnp.zeros((120, TOKENS), f32)], axis=0))
    for e in range(EXITS):
        block = logits[e * TOKENS : (e + 1) * TOKENS, :]
        log_total = turned_rows[:, e : e + 1]
        grad = (jnp.exp(block - log_total) - weight) * (loss_scale / TOKENS)
        dlogit[e * TOKENS : (e + 1) * TOKENS, :] = grad.astype(bf16)

    def exchange(k):
        yk, xk = lax.div(k, 2), lax.rem(k, 2)
        return pltpu.make_async_remote_copy(
            src_ref=partial.at[yk, xk, :, :, :, 1 - c],
            dst_ref=swapped.at[yk, xk],
            send_sem=swap_send.at[k],
            recv_sem=swap_recv.at[k],
            device_id=partner,
            device_id_type=MESH,
        )

    def fold(k, _):
        part = lax.dot_general(
            dlogit[...], head[head_rows(k), :], (((1,), (1,)), ((), ())), preferred_element_type=f32
        )
        shape = (EXITS, 4, 2, 2, ROWS, width)
        partial[lax.div(k, 2), lax.rem(k, 2)] = part.astype(bf16).reshape(shape)
        exchange(k).start()
        return 0

    def add_swapped(k, _):
        yk, xk = lax.div(k, 2), lax.rem(k, 2)
        exchange(k).wait_recv()
        for e in range(EXITS):
            for low in range(2):
                mine = partial[yk, xk, e, :, low, c].astype(f32)
                theirs = swapped[yk, xk, e, :, low].astype(f32)
                partial[yk, xk, e, :, low, c] = (mine + theirs).astype(bf16)
        return 0

    def outer(k, _):
        part = lax.dot_general(
            rows_of(k), dlogit[...], (((0,), (0,)), ((), ())), preferred_element_type=f32
        )
        grad_head[head_rows(k), :] = part.astype(bf16)
        return 0

    lax.fori_loop(0, 8, fold, 0)
    lax.fori_loop(0, 8, add_swapped, 0)
    terms = rows[EXITS : 2 * EXITS] + rows[:EXITS] * rows[2 * EXITS : 2 * EXITS + 1]
    mean = jnp.sum(terms, axis=1, keepdims=True) / TOKENS
    divergence[...] = jnp.broadcast_to(mean, (EXITS, 128))

    def add(e, axis, at, whole, part, arrived):
        dims = whole_dims(whole)

        def step(n, _):
            index = split_x({**pos, axis: at})
            found = []
            for d, size in reversed(dims):
                index[d] = lax.rem(n, size)
                found.insert(0, index[d])
                n = lax.div(n, size)
            ref = partial.at[
                index["y"], index["xh"], e, index["z"], index["xl"], c, :, columns_of(part)
            ]
            total = ref[...].astype(f32)
            for slot in arrived:
                total = total + slot[tuple(found)].astype(f32)
            ref[...] = total.astype(bf16)
            return 0

        lax.fori_loop(0, 4 ** len(whole), step, 0)

    def sums(turn, slots, between):
        went = []
        for e in range(EXITS):
            axis, whole = ORDER[e][2 - turn], ORDER[e][: 2 - turn]
            here = pos[axis]
            after, _, before = around(axis)
            up, far, down = (turned(here, k) for k in (1, 2, 3))
            went.append(
                [
                    copies.start(region(partial, e, {axis: far}, whole, 0), slots[e].at[0], after),
                    copies.start(region(partial, e, {axis: far}, whole, 1), slots[e].at[1], before),
                    copies.start(region(partial, e, {axis: up}, whole, 1), slots[e].at[3], after),
                    copies.start(region(partial, e, {axis: down}, whole, 0), slots[e].at[4], before),
                ]
            )
        between(0)
        for e in range(EXITS):
            axis, whole = ORDER[e][2 - turn], ORDER[e][: 2 - turn]
            here = pos[axis]
            after, _, before = around(axis)
            up, down = turned(here, 1), turned(here, 3)
            went[e][0].wait_recv()
            add(e, axis, up, whole, 0, [slots[e].at[0]])
            block = region(partial, e, {axis: up}, whole, 0)
            went[e].append(copies.start(block, slots[e].at[2], after))
            went[e][1].wait_recv()
            add(e, axis, down, whole, 1, [slots[e].at[1]])
            block = region(partial, e, {axis: down}, whole, 1)
            went[e].append(copies.start(block, slots[e].at[5], before))
        between(1)
        for e in range(EXITS):
            axis, whole = ORDER[e][2 - turn], ORDER[e][: 2 - turn]
            for k in range(2, 6):
                went[e][k].wait_recv()
            for part in range(2):
                add(e, axis, pos[axis], whole, part, [slots[e].at[2 + part], slots[e].at[4 + part]])

    def some_outer(n):
        lax.fori_loop((0, 6)[n], (6, 8)[n], outer, 0)

    sums(0, (first_0, first_1, first_2), some_outer)
    sums(1, (second_0, second_1, second_2), lambda n: None)
    went = []
    for e in range(EXITS):
        axis = ORDER[e][0]
        for k, there in enumerate(around(axis)):
            block = region(partial, e, {axis: turned(pos[axis], k + 1)}, (), None)
            went.append(copies.start(block, third.at[e, k], there))
    inner_sums = []
    for e in range(EXITS):
        total = partial[y, xh, e, z, xl, c].astype(f32)
        for k in range(3):
            went[3 * e + k].wait_recv()
            total = total + third[e, k].astype(f32)
        weighted = gain[e : e + 1, :] * total
        summed[e] = weighted
        inner_sums.append(jnp.sum(weighted * hidden[e].astype(f32), axis=1, keepdims=True))
    inner_slots[s] = by_lane(inner_sums, ROWS)
    to_all(copies, inner_slots, s, section_peers(s, v))
    inner = slots_sum(inner_slots, 8)
    cube = inverse[...] * inverse[...] * inverse[...] * inner / (8 * width)
    for e in range(EXITS):
        scale = column_of(inverse[...], e)
        back = scale * summed[e] - hidden[e].astype(f32) * column_of(cube, e)
        grad_hidden[e] = back.astype(bf16)
    copies.finish()
    for k in range(8):
        exchange(k).wait_send()


def body(exit_hidden, norm_gain, head_weight, teacher):
    width, cols = exit_hidden.shape[2], head_weight.shape[1]
    half = width // 2
    vmem = pl.BlockSpec(memory_space=pltpu.VMEM)
    hbm = pl.BlockSpec(memory_space=pltpu.HBM)
    dma = pltpu.SemaphoreType.DMA
    tile = (4, 2, EXITS, 4, 2, 2, ROWS, width)
    divergence, grad_hidden, grad_head = pl.pallas_call(
        kernel,
        out_shape=(
            jax.ShapeDtypeStruct((EXITS, 128), f32),
            jax.ShapeDtypeStruct(exit_hidden.shape, bf16),
            pltpu.VMEM(head_weight.shape, bf16),
        ),
        in_specs=[hbm] * 4,
        out_specs=(vmem,) * 3,
        scratch_shapes=[
            pltpu.VMEM(exit_hidden.shape, bf16),
            pltpu.VMEM(norm_gain.shape, f32),
            pltpu.VMEM(teacher.shape, f32),
            pltpu.VMEM(tile, bf16),
            pltpu.VMEM(head_weight.shape, bf16),
            pltpu.VMEM((EXITS * TOKENS, cols), f32),
            pltpu.VMEM((16, ROWS, cols), f32),
            pltpu.VMEM((EXITS * TOKENS, cols), bf16),
            pltpu.VMEM((ROWS, 128), f32),
            pltpu.VMEM(exit_hidden.shape, f32),
            pltpu.VMEM(tile, bf16),
            pltpu.VMEM((4, 2, EXITS, 4, 2, ROWS, width), bf16),
        ]
        + [
            pltpu.VMEM((6, *(n for _, n in whole_dims(ORDER[e][:whole])), ROWS, half), bf16)
            for whole in (2, 1)
            for e in range(EXITS)
        ]
        + [
            pltpu.VMEM((EXITS, 3, ROWS, width), bf16),
            pltpu.VMEM((8, ROWS, 128), f32),
            pltpu.VMEM((16, 8, TOKENS), f32),
            pltpu.VMEM((8, 8, TOKENS), f32),
            pltpu.VMEM((8, ROWS, 128), f32),
            dma((162,)),
            dma((162,)),
            dma((8,)),
            dma((8,)),
            dma((4,)),
        ],
        compiler_params=pltpu.CompilerParams(
            collective_id=0, has_side_effects=True, vmem_limit_bytes=53 * 2**20
        ),
        name="exits",
    )(exit_hidden, norm_gain, teacher, head_weight)
    return divergence[:, 0], grad_hidden, grad_head


def solution(mesh):
    return jax.shard_map(
        body,
        mesh=mesh,
        in_specs=(
            P(None, "vocab", "section"),
            P(None, "section"),
            P(None, ("section", "vocab")),
            P("vocab", "section"),
        ),
        out_specs=(P(), P(None, "vocab", "section"), P(None, ("section", "vocab"))),
        check_vma=False,
    )
```

time: 147 us -> 124 us (0.84)
  matrix products: 14.1 us -> 0 us
  Pallas kernels: 127 us -> 118 us
    dot_general x1 -> x0, matrix products: 14.1 us -> none  [body(): lax.dot_general(full.reshape(8, EXITS * TOKENS, width), dlogit, (((1,), (...]
    pallas_call x2 -> x1, Pallas kernels: 127 us -> 118 us  [body(): pl.pallas_call(kernel, out_shape=(jax.ShapeDtypeStruct((EXITS, 128), f32)...]
    unnamed x13 -> x4, local copies, waits for them, and re-layouts: 4.09 us -> 4.04 us
where the time goes in v2:
time: 124 us
  Pallas kernels  118 us (95%)
  local copies, waits for them, and re-layouts  5.35 us (4%)
    pallas_call x1, Pallas kernels, body(): pl.pallas_call(kernel, out_shape=(jax.ShapeDtypeStruct((EXITS, 128), f32)...  118 us
    unnamed x4, local copies, waits for them, and re-layouts  4.04 us

profile of v2, /device:TPU:0, one launch (start us, length us, event | category | flops | bytes accessed | tf_op | source)
XLA Modules:
  0.0 124.2 jit_solution(1805330210451943068)
XLA Ops:
  0.6 118.2 %exits.1 = (f32[3,128]{1,0:T(4,128)}, bf16[3,16,1024]{2,1,0:T(8,128)(2,1)}, bf16[8192,512]{1,0:T(8,128)(2,1)S(1)}) custom-call(bf16[3,16,1024]{2,1,0:T(8,128)(2,1)} %hidden_hbm.1, f32[3,1024]{1,0:T(4,128)} %gain_hbm.1, f32[16,8192]{1,0:T(8,128)} %teacher_hbm.1, bf16[8192,512]{1,0:T(8,128)(2,1)} %head_hbm.1), custom_call_target="tpu_custom_call" | custom-call | tf_op jit(solution)/shard_map/exits/pallas_call | solution.py:438
  118.8 1.3 %slice_reduce_fusion = f32[3]{0:T(128)} fusion(f32[3,128]{1,0:T(4,128)} %get-tuple-element.6), kind=kLoop, calls=%fused_computation | loop fusion | bytes 24 | tf_op jit(solution)/shard_map/slice | solution.py:483
  120.1 0.0 copy-start
  120.1 3.4 %copy.9 = bf16[8192,512]{1,0:T(8,128)(2,1)} copy(bf16[8192,512]{1,0:T(8,128)(2,1)S(1)} %get-tuple-element.11) | data formatting | bytes 16777216
  123.5 0.0 copy-done
  123.5 0.6 copy.10
Async XLA Ops:
  120.1 3.4 %copy-start = (bf16[3,16,1024]{2,1,0:T(8,128)(2,1)S(1)}, bf16[3,16,1024]{2,1,0:T(8,128)(2,1)}, u32[]{:S(2)}) copy-start(bf16[3,16,1024]{2,1,0:T(8,128)(2,1)} %get-tuple-element.16) | copy-start | bytes 294916

commit v3 on v2

--- a/solution.py
+++ b/solution.py
@@ -184,10 +184,45 @@
     def around(axis):
         return [neighbour(pos, c, axis, by) for by in (1, 2, 3)]
 
-    swaps = []
-
     def swap(ref):
-        swaps.append(copies.start(ref, ref, partner))
+        return copies.start(ref, ref, partner)
+
+    def rows_of(k):
+        return full[lax.div(k, 2), lax.rem(k, 2)].reshape(EXITS * TOKENS, width)
+
+    def head_rows(k):
+        return pl.ds(pl.multiple_of(k * width, 128), width)
+
+    def across_x(by):
+        there = turned(x, by)
+        high, low = lax.div(there, 2), lax.rem(there, 2)
+
+        def step(k, _):
+            tokens = full[k, high, 0, :, low].reshape(TOKENS // 2, width)
+            part = jnp.dot(tokens, head[head_rows(2 * k + high), :], preferred_element_type=f32)
+            logits[0, :, low] += part.reshape(4, 2, ROWS, cols)
+            return 0
+
+        lax.fori_loop(0, 4, step, 0)
+
+    def across_y(by):
+        there = turned(y, by)
+
+        def step(k, _):
+            tokens = full[there, k, 1].reshape(TOKENS, width)
+            part = jnp.dot(tokens, head[head_rows(2 * there + k), :], preferred_element_type=f32)
+            logits[1] += part.reshape(4, 2, 2, ROWS, cols)
+            return 0
+
+        lax.fori_loop(0, 2, step, 0)
+
+    def last_exit(k, _):
+        tokens = full[lax.div(k, 2), lax.rem(k, 2), 2].reshape(TOKENS, width)
+        part = jnp.dot(tokens, head[head_rows(k), :], preferred_element_type=f32)
+        logits[2] += part.reshape(4, 2, 2, ROWS, cols)
+        return 0
+
+    logits[...] = jnp.zeros(logits.shape, f32)
 
     sent = []
     for e in range(EXITS):
@@ -208,8 +243,13 @@
             down_low = copies.start(low, low, before)
             pieces.append((up_low, down_high, up_high, down_low))
         if last:
-            for e in range(EXITS):
-                swap(region(full, e, {}, ORDER[e][:2], None))
+            own_swaps = [swap(region(full, e, {}, ORDER[e][:2], None)) for e in range(EXITS)]
+            near_swaps = [[], [], []]
+            far_swaps = [[], [], [own_swaps[2]]]
+            loads[2].wait()
+            for e in range(2):
+                own_swaps[e].wait_recv()
+                (across_x, across_y)[e](0)
         relays = []
         for e in range(EXITS):
             axis, whole = ORDER[e][turn], ORDER[e][:turn]
@@ -219,21 +259,21 @@
             block = region(full, e, {axis: turned(pos[axis], 3)}, whole, 0)
             up = copies.start(block, block, after)
             if last:
-                swap(block)
+                near_swaps[e].append(swap(block))
             down_high.wait_recv()
             block = region(full, e, {axis: turned(pos[axis], 1)}, whole, 1)
             down = copies.start(block, block, before)
             if last:
-                swap(block)
+                near_swaps[e].append(swap(block))
             relays.append((up, down))
         for e in range(EXITS):
             axis, whole = ORDER[e][turn], ORDER[e][:turn]
             pieces[e][2].wait_recv()
             if last:
-                swap(region(full, e, {axis: turned(pos[axis], 3)}, whole, 1))
+                near_swaps[e].append(swap(region(full, e, {axis: turned(pos[axis], 3)}, whole, 1)))
             pieces[e][3].wait_recv()
             if last:
-                swap(region(full, e, {axis: turned(pos[axis], 1)}, whole, 0))
+                near_swaps[e].append(swap(region(full, e, {axis: turned(pos[axis], 1)}, whole, 0)))
         if last:
             loads[3].wait()
             lent = [
@@ -245,41 +285,38 @@
                 for peer in vocab_peers(s, v)
             ]
             target[v] = teacher[:, pl.ds(pl.multiple_of(v * cols, 128), cols)]
+            for e in range(2):
+                for copy in near_swaps[e]:
+                    copy.wait_recv()
+                (across_x, across_y)[e](1)
+                (across_x, across_y)[e](3)
+            far_swaps[2] += near_swaps[2]
         for e in range(EXITS):
             axis, whole = ORDER[e][turn], ORDER[e][:turn]
             for k in range(2):
                 relays[e][k].wait_recv()
                 if last:
-                    swap(region(full, e, {axis: turned(pos[axis], 2)}, whole, k))
-    for copy in swaps:
-        copy.wait_recv()
-    loads[2].wait()
-
-    logits[...] = jnp.zeros(logits.shape, f32)
-
-    def rows_of(k):
-        return full[lax.div(k, 2), lax.rem(k, 2)].reshape(EXITS * TOKENS, width)
-
-    def head_rows(k):
-        return pl.ds(pl.multiple_of(k * width, 128), width)
-
-    def multiply(k, _):
-        logits[...] += jnp.dot(rows_of(k), head[head_rows(k), :], preferred_element_type=f32)
-        return 0
-
-    lax.fori_loop(0, 8, multiply, 0)
+                    block = region(full, e, {axis: turned(pos[axis], 2)}, whole, k)
+                    far_swaps[e].append(swap(block))
+    for e in range(EXITS):
+        axis, whole = ORDER[e][2], ORDER[e][:2]
+        for copy in far_swaps[e]:
+            copy.wait_recv()
+        if e < 2:
+            (across_x, across_y)[e](2)
+    lax.fori_loop(0, 8, last_exit, 0)
     for copy in lent:
         copy.wait_recv()
 
     columns = []
     for e in range(EXITS):
-        block = logits[e * TOKENS : (e + 1) * TOKENS, :]
+        block = logits[e].reshape(TOKENS, cols)
         top = jnp.max(block, axis=1, keepdims=True)
         columns.append(top + jnp.log(jnp.sum(jnp.exp(block - top), axis=1, keepdims=True)))
     stored = target[...].reshape(TOKENS, cols)
     weight = jnp.exp(stored)
     for e in range(EXITS):
-        block = logits[e * TOKENS : (e + 1) * TOKENS, :]
+        block = logits[e].reshape(TOKENS, cols)
         columns.append(jnp.sum(weight * (stored - block), axis=1, keepdims=True))
     columns.append(jnp.sum(weight, axis=1, keepdims=True))
     vocab_slots[v] = jnp.transpose(by_lane(columns, TOKENS))[:8]
@@ -289,13 +326,16 @@
     rows = merged(section_slots, 8)
     turned_rows = jnp.transpose(jnp.concatenate([rows, jnp.zeros((120, TOKENS), f32)], axis=0))
     for e in range(EXITS):
-        block = logits[e * TOKENS : (e + 1) * TOKENS, :]
+        block = logits[e].reshape(TOKENS, cols)
         log_total = turned_rows[:, e : e + 1]
         grad = (jnp.exp(block - log_total) - weight) * (loss_scale / TOKENS)
         dlogit[e * TOKENS : (e + 1) * TOKENS, :] = grad.astype(bf16)
 
+    def fold_place(k):
+        return lax.rem(y + lax.rem(k, 4), 4), lax.rem(xh + 1 - lax.div(k, 4), 2)
+
     def exchange(k):
-        yk, xk = lax.div(k, 2), lax.rem(k, 2)
+        yk, xk = fold_place(k)
         return pltpu.make_async_remote_copy(
             src_ref=partial.at[yk, xk, :, :, :, 1 - c],
             dst_ref=swapped.at[yk, xk],
@@ -306,16 +346,18 @@
         )
 
     def fold(k, _):
+        yk, xk = fold_place(k)
+        rows = head[head_rows(2 * yk + xk), :]
         part = lax.dot_general(
-            dlogit[...], head[head_rows(k), :], (((1,), (1,)), ((), ())), preferred_element_type=f32
+            dlogit[...], rows, (((1,), (1,)), ((), ())), preferred_element_type=f32
         )
         shape = (EXITS, 4, 2, 2, ROWS, width)
-        partial[lax.div(k, 2), lax.rem(k, 2)] = part.astype(bf16).reshape(shape)
+        partial[yk, xk] = part.astype(bf16).reshape(shape)
         exchange(k).start()
         return 0
 
     def add_swapped(k, _):
-        yk, xk = lax.div(k, 2), lax.rem(k, 2)
+        yk, xk = fold_place(k)
         exchange(k).wait_recv()
         for e in range(EXITS):
             for low in range(2):
@@ -331,8 +373,6 @@
         grad_head[head_rows(k), :] = part.astype(bf16)
         return 0
 
-    lax.fori_loop(0, 8, fold, 0)
-    lax.fori_loop(0, 8, add_swapped, 0)
     terms = rows[EXITS : 2 * EXITS] + rows[:EXITS] * rows[2 * EXITS : 2 * EXITS + 1]
     mean = jnp.sum(terms, axis=1, keepdims=True) / TOKENS
     divergence[...] = jnp.broadcast_to(mean, (EXITS, 128))
@@ -358,48 +398,90 @@
 
         lax.fori_loop(0, 4 ** len(whole), step, 0)
 
-    def sums(turn, slots, between):
-        went = []
-        for e in range(EXITS):
-            axis, whole = ORDER[e][2 - turn], ORDER[e][: 2 - turn]
-            here = pos[axis]
+    def first_copies(e, axis, whole, slots):
+        after, _, before = around(axis)
+        up, far, down = (turned(pos[axis], k) for k in (1, 2, 3))
+        return [
+            copies.start(region(partial, e, {axis: far}, whole, 0), slots.at[0], after),
+            copies.start(region(partial, e, {axis: far}, whole, 1), slots.at[1], before),
+            copies.start(region(partial, e, {axis: up}, whole, 1), slots.at[3], after),
+            copies.start(region(partial, e, {axis: down}, whole, 0), slots.at[4], before),
+        ]
+
+    def first_group(group):
+        high = lax.rem(xh + 1 - group, 2)
+        went = [[], [], []]
+        if group == 0:
+            after, _, before = around("x")
+            for part, there in ((0, after), (1, before)):
+                block = region(partial, 0, {"x": turned(x, 2)}, ("y", "z"), part)
+                went[0].append(copies.start(block, first_0.at[part], there))
+        side = xl if group == 0 else 1 - xl
+        by = 3 + 2 * side
+        block = partial.at[
+            :, high, 0, :, 1 - xl, c, :, pl.ds(pl.multiple_of(side * half, 128), half)
+        ]
+        went[0].append(copies.start(block, first_0.at[4 - side], neighbour(pos, c, "x", by)))
+        for e, axis, slots in ((1, "y", first_1), (2, "z", first_2)):
             after, _, before = around(axis)
-            up, far, down = (turned(here, k) for k in (1, 2, 3))
-            went.append(
-                [
-                    copies.start(region(partial, e, {axis: far}, whole, 0), slots[e].at[0], after),
-                    copies.start(region(partial, e, {axis: far}, whole, 1), slots[e].at[1], before),
-                    copies.start(region(partial, e, {axis: up}, whole, 1), slots[e].at[3], after),
-                    copies.start(region(partial, e, {axis: down}, whole, 0), slots[e].at[4], before),
-                ]
-            )
-        between(0)
-        for e in range(EXITS):
-            axis, whole = ORDER[e][2 - turn], ORDER[e][: 2 - turn]
-            here = pos[axis]
-            after, _, before = around(axis)
-            up, down = turned(here, 1), turned(here, 3)
-            went[e][0].wait_recv()
-            add(e, axis, up, whole, 0, [slots[e].at[0]])
-            block = region(partial, e, {axis: up}, whole, 0)
-            went[e].append(copies.start(block, slots[e].at[2], after))
-            went[e][1].wait_recv()
-            add(e, axis, down, whole, 1, [slots[e].at[1]])
-            block = region(partial, e, {axis: down}, whole, 1)
-            went[e].append(copies.start(block, slots[e].at[5], before))
-        between(1)
-        for e in range(EXITS):
-            axis, whole = ORDER[e][2 - turn], ORDER[e][: 2 - turn]
-            for k in range(2, 6):
-                went[e][k].wait_recv()
-            for part in range(2):
-                add(e, axis, pos[axis], whole, part, [slots[e].at[2 + part], slots[e].at[4 + part]])
-
-    def some_outer(n):
-        lax.fori_loop((0, 6)[n], (6, 8)[n], outer, 0)
-
-    sums(0, (first_0, first_1, first_2), some_outer)
-    sums(1, (second_0, second_1, second_2), lambda n: None)
+            up, far, down = (turned(pos[axis], k) for k in (1, 2, 3))
+            plan = ((far, 0, 0, after), (far, 1, 1, before), (up, 1, 3, after), (down, 0, 4, before))
+            for at, part, slot, there in plan:
+                place_z = slice(None) if axis == "y" else at
+                place_y = at if axis == "y" else slice(None)
+                block = partial.at[place_y, high, e, place_z, :, c, :, columns_of(part)]
+                into = slots.at[slot, high] if axis == "y" else slots.at[slot, :, high]
+                went[e].append(copies.start(block, into, there))
+        return went
+
+    def relay(e, axis, whole, slots, low, high):
+        after, _, before = around(axis)
+        up, down = turned(pos[axis], 1), turned(pos[axis], 3)
+        for copy in low:
+            copy.wait_recv()
+        add(e, axis, up, whole, 0, [slots.at[0]])
+        block = region(partial, e, {axis: up}, whole, 0)
+        sent = [copies.start(block, slots.at[2], after)]
+        for copy in high:
+            copy.wait_recv()
+        add(e, axis, down, whole, 1, [slots.at[1]])
+        block = region(partial, e, {axis: down}, whole, 1)
+        return sent + [copies.start(block, slots.at[5], before)]
+
+    def last_sums(e, axis, whole, slots, waits):
+        for copy in waits:
+            copy.wait_recv()
+        for part in range(2):
+            add(e, axis, pos[axis], whole, part, [slots.at[2 + part], slots.at[4 + part]])
+
+    first = (first_0, first_1, first_2)
+    lax.fori_loop(0, 5, fold, 0)
+    lax.fori_loop(0, 4, add_swapped, 0)
+    near_half = first_group(0)
+    lax.fori_loop(5, 8, fold, 0)
+    lax.fori_loop(4, 8, add_swapped, 0)
+    own_half = first_group(1)
+    lax.fori_loop(0, 5, outer, 0)
+    waits = []
+    for e in range(EXITS):
+        one, two = near_half[e], own_half[e]
+        if e == 0:
+            low, high, rest = one[:1], one[1:2], one[2:] + two
+        else:
+            low, high, rest = [one[0], two[0]], [one[1], two[1]], one[2:] + two[2:]
+        waits.append(rest + relay(e, ORDER[e][2], ORDER[e][:2], first[e], low, high))
+    lax.fori_loop(5, 8, outer, 0)
+    for e in range(EXITS):
+        last_sums(e, ORDER[e][2], ORDER[e][:2], first[e], waits[e])
+    second = (second_0, second_1, second_2)
+    began = [first_copies(e, ORDER[e][1], ORDER[e][:1], second[e]) for e in range(EXITS)]
+    waits = []
+    for e in range(EXITS):
+        low, high = began[e][:1], began[e][1:2]
+        sent = relay(e, ORDER[e][1], ORDER[e][:1], second[e], low, high)
+        waits.append(began[e][2:] + sent)
+    for e in range(EXITS):
+        last_sums(e, ORDER[e][1], ORDER[e][:1], second[e], waits[e])
     went = []
     for e in range(EXITS):
         axis = ORDER[e][0]
@@ -450,7 +532,7 @@
             pltpu.VMEM(teacher.shape, f32),
             pltpu.VMEM(tile, bf16),
             pltpu.VMEM(head_weight.shape, bf16),
-            pltpu.VMEM((EXITS * TOKENS, cols), f32),
+            pltpu.VMEM((EXITS, 4, 2, 2, ROWS, cols), f32),
             pltpu.VMEM((16, ROWS, cols), f32),
             pltpu.VMEM((EXITS * TOKENS, cols), bf16),
             pltpu.VMEM((ROWS, 128), f32),
@@ -469,8 +551,8 @@
             pltpu.VMEM((16, 8, TOKENS), f32),
             pltpu.VMEM((8, 8, TOKENS), f32),
             pltpu.VMEM((8, ROWS, 128), f32),
-            dma((162,)),
-            dma((162,)),
+            dma((172,)),
+            dma((172,)),
             dma((8,)),
             dma((8,)),
             dma((4,)),

time: 124 us -> 119 us (0.960)
  Pallas kernels: 118 us -> 113 us
    pallas_call x1, Pallas kernels: 118 us -> 113 us  [body(): pl.pallas_call(kernel, out_shape=(jax.ShapeDtypeStruct((EXITS, 128), f32)...]
where the time goes in v3:
time: 119 us
  Pallas kernels  113 us (95%)
  local copies, waits for them, and re-layouts  5.35 us (4%)
    pallas_call x1, Pallas kernels, body(): pl.pallas_call(kernel, out_shape=(jax.ShapeDtypeStruct((EXITS, 128), f32)...  113 us
    unnamed x4, local copies, waits for them, and re-layouts  4.04 us

profile of v3, /device:TPU:0, one launch (start us, length us, event | category | flops | bytes accessed | tf_op | source)
XLA Modules:
  0.0 118.8 jit_solution(14650888997718591174)
XLA Ops:
  0.6 112.8 %exits.1 = (f32[3,128]{1,0:T(4,128)}, bf16[3,16,1024]{2,1,0:T(8,128)(2,1)}, bf16[8192,512]{1,0:T(8,128)(2,1)S(1)}) custom-call(bf16[3,16,1024]{2,1,0:T(8,128)(2,1)} %hidden_hbm.1, f32[3,1024]{1,0:T(4,128)} %gain_hbm.1, f32[16,8192]{1,0:T(8,128)} %teacher_hbm.1, bf16[8192,512]{1,0:T(8,128)(2,1)} %head_hbm.1), custom_call_target="tpu_custom_call" | custom-call | tf_op jit(solution)/shard_map/exits/pallas_call | solution.py:520
  113.4 1.3 %slice_reduce_fusion = f32[3]{0:T(128)} fusion(f32[3,128]{1,0:T(4,128)} %get-tuple-element.6), kind=kLoop, calls=%fused_computation | loop fusion | bytes 24 | tf_op jit(solution)/shard_map/slice | solution.py:565
  114.7 0.0 copy-start
  114.7 3.4 %copy.9 = bf16[8192,512]{1,0:T(8,128)(2,1)} copy(bf16[8192,512]{1,0:T(8,128)(2,1)S(1)} %get-tuple-element.11) | data formatting | bytes 16777216
  118.1 0.0 copy-done
  118.1 0.6 copy.10
Async XLA Ops:
  114.7 3.4 %copy-start = (bf16[3,16,1024]{2,1,0:T(8,128)(2,1)S(1)}, bf16[3,16,1024]{2,1,0:T(8,128)(2,1)}, u32[]{:S(2)}) copy-start(bf16[3,16,1024]{2,1,0:T(8,128)(2,1)} %get-tuple-element.16) | copy-start | bytes 294916

commit v4 on v3

--- a/solution.py
+++ b/solution.py
@@ -35,7 +35,7 @@
 
 class Copies:
     def __init__(self, send_sem, recv_sem):
-        self.send_sem, self.recv_sem, self.made = send_sem, recv_sem, []
+        self.send_sem, self.recv_sem, self.made, self.left = send_sem, recv_sem, [], 0
 
     def start(self, src, dst, device):
         n = len(self.made)
@@ -52,8 +52,9 @@
         return copy
 
     def finish(self):
-        for copy in self.made:
+        for copy in self.made[self.left :]:
             copy.wait_send()
+        self.left = len(self.made)
 
 
 def neighbour(pos, c, axis, by):
@@ -93,10 +94,17 @@
     return [(d, n) for d, n in DIMS if d[0] in whole]
 
 
-def to_all(copies, slots, me, peers):
-    sent = [copies.start(slots.at[me], slots.at[me], peer) for peer in peers]
+def begin(copies, slots, me, peers):
+    return [copies.start(slots.at[me], slots.at[me], peer) for peer in peers]
+
+
+def wait_for(sent):
     for copy in sent:
         copy.wait_recv()
+
+
+def to_all(copies, slots, me, peers):
+    wait_for(begin(copies, slots, me, peers))
 
 
 def by_lane(columns, rows):
@@ -135,9 +143,10 @@
 
 def kernel(
     hidden_hbm, gain_hbm, teacher_hbm, head_hbm, divergence, grad_hidden, grad_head,
-    hidden, gain, teacher, full, head, logits, target, dlogit, inverse, summed, partial, swapped,
+    hidden, gain, teacher, full, head, logits, target, dlogit, inverse, partial, swapped,
     first_0, first_1, first_2, second_0, second_1, second_2, third,
-    square_slots, vocab_slots, section_slots, inner_slots,
+    square_slots, vocab_slots, section_slots, gain_slots, inverse_slots, inner_vocab, inner_section,
+    inner_rows,
     send_sem, recv_sem, swap_send, swap_recv, local_sem,
 ):
     width, cols = hidden.shape[2], head.shape[1]
@@ -147,9 +156,9 @@
     xh, xl = lax.div(x, 2), lax.rem(x, 2)
     partner = chip(**pos, c=1 - c)
     copies = Copies(send_sem, recv_sem)
-    near = [neighbour(pos, c, "x", by) for by in (1, 3)]
-    near += [neighbour(pos, c, "z", by) for by in (1, 2, 3)]
-    ready = greet([partner] + section_peers(s, v) + near)
+    same_core = [(s, lax.rem(v + k, 16)) for k in range(2, 16, 2)]
+    beyond = neighbour(pos, c, "x", 3 + 2 * xl)
+    ready = greet([partner, beyond] + section_peers(s, v) + same_core)
     loads = [
         pltpu.make_async_copy(src, dst, local_sem.at[k])
         for k, (src, dst) in enumerate(
@@ -163,14 +172,12 @@
         jnp.sum(jnp.square(hidden[e].astype(f32)), axis=1, keepdims=True) for e in range(EXITS)
     ]
     square_slots[s] = by_lane(squares, ROWS)
+    for e in range(EXITS):
+        full[y, xh, e, z, xl, c] = hidden[e]
     loads[1].wait()
+    gain_slots[s] = gain[...]
     ready()
-    to_all(copies, square_slots, s, section_peers(s, v))
-    inverse[...] = lax.rsqrt(slots_sum(square_slots, 8) / (8 * width) + epsilon)
-    for e in range(EXITS):
-        scale = column_of(inverse[...], e)
-        normed = hidden[e].astype(f32) * scale * gain[e : e + 1, :]
-        full[y, xh, e, z, xl, c] = normed.astype(bf16)
+    square_copies = begin(copies, square_slots, s, section_peers(s, v))
 
     def columns_of(part):
         return slice(None) if part is None else slice(part * half, (part + 1) * half)
@@ -228,11 +235,39 @@
     for e in range(EXITS):
         mine = region(full, e, {}, (), None)
         sent += [copies.start(mine, mine, there) for there in around(ORDER[e][0])]
-    for copy in sent:
-        copy.wait_recv()
+    gain_copies = [copies.start(gain, gain_slots.at[s], peer) for peer in section_peers(s, v)]
+    wait_for(sent)
+
+    def normalise(block, scale, gains):
+        block[...] = (block[...].astype(f32) * scale * gains).astype(bf16)
+
+    def normalise_step(k, _):
+        for n in range(4):
+            high, low = divmod(n, 2)
+            normalise(
+                full.at[k, xh, 0, n, xl, c],
+                inverse_slots[2 * n + xl][:, 0:1],
+                gain_slots[2 * k + xh][0:1, :],
+            )
+            normalise(
+                full.at[y, high, 1, k, low, c],
+                inverse_slots[2 * k + low][:, 1:2],
+                gain_slots[2 * y + high][1:2, :],
+            )
+            normalise(
+                full.at[k, high, 2, z, low, c],
+                inverse_slots[2 * z + low][:, 2:3],
+                gain_slots[2 * k + high][2:3, :],
+            )
+        return 0
+
     for turn in (1, 2):
         last = turn == 2
         pieces = []
+        if last:
+            wait_for(gain_copies + inverse_copies)
+            copies.finish()
+            lax.fori_loop(0, 4, normalise_step, 0)
         for e in range(EXITS):
             axis, whole = ORDER[e][turn], ORDER[e][:turn]
             after, _, before = around(axis)
@@ -250,6 +285,11 @@
             for e in range(2):
                 own_swaps[e].wait_recv()
                 (across_x, across_y)[e](0)
+        else:
+            wait_for(square_copies)
+            inverse[...] = lax.rsqrt(slots_sum(square_slots, 8) / (8 * width) + epsilon)
+            inverse_slots[lax.div(v, 2)] = inverse[...]
+            inverse_copies = begin(copies, inverse_slots, lax.div(v, 2), same_core)
         relays = []
         for e in range(EXITS):
             axis, whole = ORDER[e][turn], ORDER[e][:turn]
@@ -461,7 +501,16 @@
     lax.fori_loop(5, 8, fold, 0)
     lax.fori_loop(4, 8, add_swapped, 0)
     own_half = first_group(1)
+    columns = []
+    for e in range(EXITS):
+        grad = dlogit[e * TOKENS : (e + 1) * TOKENS, :].astype(f32)
+        columns.append(jnp.sum(grad * logits[e].reshape(TOKENS, cols), axis=1, keepdims=True))
+    inner_vocab[v] = jnp.transpose(by_lane(columns, TOKENS))[:8]
+    inner_copies = begin(copies, inner_vocab, v, vocab_peers(s, v))
     lax.fori_loop(0, 5, outer, 0)
+    wait_for(inner_copies)
+    inner_section[s] = slots_sum(inner_vocab, 16)
+    inner_copies = begin(copies, inner_section, s, section_peers(s, v))
     waits = []
     for e in range(EXITS):
         one, two = near_half[e], own_half[e]
@@ -473,6 +522,9 @@
     lax.fori_loop(5, 8, outer, 0)
     for e in range(EXITS):
         last_sums(e, ORDER[e][2], ORDER[e][:2], first[e], waits[e])
+    wait_for(inner_copies)
+    inner = slots_sum(inner_section, 8)
+    inner_rows[...] = jnp.transpose(jnp.concatenate([inner, jnp.zeros((120, TOKENS), f32)], axis=0))
     second = (second_0, second_1, second_2)
     began = [first_copies(e, ORDER[e][1], ORDER[e][:1], second[e]) for e in range(EXITS)]
     waits = []
@@ -482,28 +534,21 @@
         waits.append(began[e][2:] + sent)
     for e in range(EXITS):
         last_sums(e, ORDER[e][1], ORDER[e][:1], second[e], waits[e])
+    own_inner = inner_rows[pl.ds(pl.multiple_of(v * ROWS, ROWS), ROWS), :]
+    removed = inverse[...] * inverse[...] * own_inner / (8 * width)
     went = []
     for e in range(EXITS):
         axis = ORDER[e][0]
         for k, there in enumerate(around(axis)):
             block = region(partial, e, {axis: turned(pos[axis], k + 1)}, (), None)
             went.append(copies.start(block, third.at[e, k], there))
-    inner_sums = []
     for e in range(EXITS):
         total = partial[y, xh, e, z, xl, c].astype(f32)
         for k in range(3):
             went[3 * e + k].wait_recv()
             total = total + third[e, k].astype(f32)
-        weighted = gain[e : e + 1, :] * total
-        summed[e] = weighted
-        inner_sums.append(jnp.sum(weighted * hidden[e].astype(f32), axis=1, keepdims=True))
-    inner_slots[s] = by_lane(inner_sums, ROWS)
-    to_all(copies, inner_slots, s, section_peers(s, v))
-    inner = slots_sum(inner_slots, 8)
-    cube = inverse[...] * inverse[...] * inverse[...] * inner / (8 * width)
-    for e in range(EXITS):
         scale = column_of(inverse[...], e)
-        back = scale * summed[e] - hidden[e].astype(f32) * column_of(cube, e)
+        back = scale * (gain[e : e + 1, :] * total) - hidden[e].astype(f32) * column_of(removed, e)
         grad_hidden[e] = back.astype(bf16)
     copies.finish()
     for k in range(8):
@@ -536,7 +581,6 @@
             pltpu.VMEM((16, ROWS, cols), f32),
             pltpu.VMEM((EXITS * TOKENS, cols), bf16),
             pltpu.VMEM((ROWS, 128), f32),
-            pltpu.VMEM(exit_hidden.shape, f32),
             pltpu.VMEM(tile, bf16),
             pltpu.VMEM((4, 2, EXITS, 4, 2, ROWS, width), bf16),
         ]
@@ -550,9 +594,13 @@
             pltpu.VMEM((8, ROWS, 128), f32),
             pltpu.VMEM((16, 8, TOKENS), f32),
             pltpu.VMEM((8, 8, TOKENS), f32),
+            pltpu.VMEM((8, *norm_gain.shape), f32),
             pltpu.VMEM((8, ROWS, 128), f32),
-            dma((172,)),
-            dma((172,)),
+            pltpu.VMEM((16, 8, TOKENS), f32),
+            pltpu.VMEM((8, 8, TOKENS), f32),
+            pltpu.VMEM((TOKENS, 128), f32),
+            dma((199,)),
+            dma((199,)),
             dma((8,)),
             dma((8,)),
             dma((4,)),

time: 119 us -> 118 us (level)
  no operation moved by 1% of the time
where the time goes in v4:
time: 118 us
  Pallas kernels  112 us (95%)
  local copies, waits for them, and re-layouts  5.35 us (5%)
    pallas_call x1, Pallas kernels, body(): pl.pallas_call(kernel, out_shape=(jax.ShapeDtypeStruct((EXITS, 128), f32)...  112 us
    unnamed x4, local copies, waits for them, and re-layouts  4.04 us

profile of v4, /device:TPU:0, one launch (start us, length us, event | category | flops | bytes accessed | tf_op | source)
XLA Modules:
  0.0 117.9 jit_solution(8953490275347355102)
XLA Ops:
  0.6 111.9 %exits.1 = (f32[3,128]{1,0:T(4,128)}, bf16[3,16,1024]{2,1,0:T(8,128)(2,1)}, bf16[8192,512]{1,0:T(8,128)(2,1)S(1)}) custom-call(bf16[3,16,1024]{2,1,0:T(8,128)(2,1)} %hidden_hbm.1, f32[3,1024]{1,0:T(4,128)} %gain_hbm.1, f32[16,8192]{1,0:T(8,128)} %teacher_hbm.1, bf16[8192,512]{1,0:T(8,128)(2,1)} %head_hbm.1), custom_call_target="tpu_custom_call" | custom-call | tf_op jit(solution)/shard_map/exits/pallas_call | solution.py:565
  112.5 1.3 %slice_reduce_fusion = f32[3]{0:T(128)} fusion(f32[3,128]{1,0:T(4,128)} %get-tuple-element.6), kind=kLoop, calls=%fused_computation | loop fusion | bytes 24 | tf_op jit(solution)/shard_map/slice | solution.py:613
  113.8 0.0 copy-start
  113.9 3.4 %copy.9 = bf16[8192,512]{1,0:T(8,128)(2,1)} copy(bf16[8192,512]{1,0:T(8,128)(2,1)S(1)} %get-tuple-element.11) | data formatting | bytes 16777216
  117.2 0.0 copy-done
  117.2 0.6 copy.10
Async XLA Ops:
  113.8 3.4 %copy-start = (bf16[3,16,1024]{2,1,0:T(8,128)(2,1)S(1)}, bf16[3,16,1024]{2,1,0:T(8,128)(2,1)}, u32[]{:S(2)}) copy-start(bf16[3,16,1024]{2,1,0:T(8,128)(2,1)} %get-tuple-element.16) | copy-start | bytes 294916

commit v5 on v4

--- a/solution.py
+++ b/solution.py
@@ -224,9 +224,38 @@
         lax.fori_loop(0, 2, step, 0)
 
     def last_exit(k, _):
-        tokens = full[lax.div(k, 2), lax.rem(k, 2), 2].reshape(TOKENS, width)
-        part = jnp.dot(tokens, head[head_rows(k), :], preferred_element_type=f32)
-        logits[2] += part.reshape(4, 2, 2, ROWS, cols)
+        yk, xk = lax.div(k, 2), lax.rem(k, 2)
+        places = [z, turned(z, 1), turned(z, 3)]
+        tokens = [full[yk, xk, 2, at].reshape(TOKENS // 4, width) for at in places]
+        rows = head[head_rows(k), :]
+        part = jnp.dot(jnp.concatenate(tokens, axis=0), rows, preferred_element_type=f32)
+        part = part.reshape(3, 2, 2, ROWS, cols)
+        for n, at in enumerate(places):
+            logits[2, at] += part[n]
+        return 0
+
+    def far_blocks(yk, xk, with_y, with_x):
+        far_x, far_z = turned(x, 2), turned(z, 2)
+        low = lax.rem(far_x, 2)
+        tokens = [full[yk, xk, 2, far_z].reshape(TOKENS // 4, width)]
+        if with_x:
+            tokens.append(full[yk, xk, 0, :, low].reshape(TOKENS // 2, width))
+        if with_y:
+            tokens.append(full[yk, xk, 1].reshape(TOKENS, width))
+        tokens = jnp.concatenate(tokens, axis=0) if len(tokens) > 1 else tokens[0]
+        part = jnp.dot(tokens, head[head_rows(2 * yk + xk), :], preferred_element_type=f32)
+        at = TOKENS // 4
+        logits[2, far_z] += part[:at].reshape(2, 2, ROWS, cols)
+        if with_x:
+            logits[0, :, low] += part[at : at + TOKENS // 2].reshape(4, 2, ROWS, cols)
+            at += TOKENS // 2
+        if with_y:
+            logits[1] += part[at:].reshape(4, 2, 2, ROWS, cols)
+
+    def far_step(k, _):
+        yk = turned(y, 3 + k)
+        far_blocks(yk, 1 - xh, False, True)
+        far_blocks(yk, xh, False, False)
         return 0
 
     logits[...] = jnp.zeros(logits.shape, f32)
@@ -280,7 +309,7 @@
         if last:
             own_swaps = [swap(region(full, e, {}, ORDER[e][:2], None)) for e in range(EXITS)]
             near_swaps = [[], [], []]
-            far_swaps = [[], [], [own_swaps[2]]]
+            far_swaps = []
             loads[2].wait()
             for e in range(2):
                 own_swaps[e].wait_recv()
@@ -330,21 +359,20 @@
                     copy.wait_recv()
                 (across_x, across_y)[e](1)
                 (across_x, across_y)[e](3)
-            far_swaps[2] += near_swaps[2]
+            wait_for([own_swaps[2]] + near_swaps[2])
+            lax.fori_loop(0, 4, last_exit, 0)
         for e in range(EXITS):
             axis, whole = ORDER[e][turn], ORDER[e][:turn]
             for k in range(2):
                 relays[e][k].wait_recv()
                 if last:
                     block = region(full, e, {axis: turned(pos[axis], 2)}, whole, k)
-                    far_swaps[e].append(swap(block))
-    for e in range(EXITS):
-        axis, whole = ORDER[e][2], ORDER[e][:2]
-        for copy in far_swaps[e]:
-            copy.wait_recv()
-        if e < 2:
-            (across_x, across_y)[e](2)
-    lax.fori_loop(0, 8, last_exit, 0)
+                    far_swaps.append(swap(block))
+    lax.fori_loop(4, 8, last_exit, 0)
+    wait_for(far_swaps)
+    far_blocks(turned(y, 2), 1 - xh, True, True)
+    far_blocks(turned(y, 2), xh, True, False)
+    lax.fori_loop(0, 3, far_step, 0)
     for copy in lent:
         copy.wait_recv()
 
@@ -420,7 +448,7 @@
     def add(e, axis, at, whole, part, arrived):
         dims = whole_dims(whole)
 
-        def step(n, _):
+        def add_one(n):
             index = split_x({**pos, axis: at})
             found = []
             for d, size in reversed(dims):
@@ -434,9 +462,13 @@
             for slot in arrived:
                 total = total + slot[tuple(found)].astype(f32)
             ref[...] = total.astype(bf16)
+
+        def step(n, _):
+            for k in range(4):
+                add_one(4 * n + k)
             return 0
 
-        lax.fori_loop(0, 4 ** len(whole), step, 0)
+        lax.fori_loop(0, 4 ** (len(whole) - 1), step, 0)
 
     def first_copies(e, axis, whole, slots):
         after, _, before = around(axis)
@@ -495,22 +527,22 @@
             add(e, axis, pos[axis], whole, part, [slots.at[2 + part], slots.at[4 + part]])
 
     first = (first_0, first_1, first_2)
+    columns = []
+    for e in range(EXITS):
+        grad = dlogit[e * TOKENS : (e + 1) * TOKENS, :].astype(f32)
+        columns.append(jnp.sum(grad * logits[e].reshape(TOKENS, cols), axis=1, keepdims=True))
+    inner_vocab[v] = jnp.transpose(by_lane(columns, TOKENS))[:8]
+    inner_copies = begin(copies, inner_vocab, v, vocab_peers(s, v))
     lax.fori_loop(0, 5, fold, 0)
+    wait_for(inner_copies)
+    inner_section[s] = slots_sum(inner_vocab, 16)
+    inner_copies = begin(copies, inner_section, s, section_peers(s, v))
     lax.fori_loop(0, 4, add_swapped, 0)
     near_half = first_group(0)
     lax.fori_loop(5, 8, fold, 0)
     lax.fori_loop(4, 8, add_swapped, 0)
     own_half = first_group(1)
-    columns = []
-    for e in range(EXITS):
-        grad = dlogit[e * TOKENS : (e + 1) * TOKENS, :].astype(f32)
-        columns.append(jnp.sum(grad * logits[e].reshape(TOKENS, cols), axis=1, keepdims=True))
-    inner_vocab[v] = jnp.transpose(by_lane(columns, TOKENS))[:8]
-    inner_copies = begin(copies, inner_vocab, v, vocab_peers(s, v))
     lax.fori_loop(0, 5, outer, 0)
-    wait_for(inner_copies)
-    inner_section[s] = slots_sum(inner_vocab, 16)
-    inner_copies = begin(copies, inner_section, s, section_peers(s, v))
     waits = []
     for e in range(EXITS):
         one, two = near_half[e], own_half[e]

time: 118 us -> 112 us (0.949)
  Pallas kernels: 112 us -> 105 us
    pallas_call x1, Pallas kernels: 112 us -> 105 us  [body(): pl.pallas_call(kernel, out_shape=(jax.ShapeDtypeStruct((EXITS, 128), f32)...]
where the time goes in v5:
time: 112 us; the launch traced here: 111 us
  Pallas kernels  105 us (94%)
  local copies, waits for them, and re-layouts  5.35 us (5%)
    pallas_call x1, Pallas kernels, body(): pl.pallas_call(kernel, out_shape=(jax.ShapeDtypeStruct((EXITS, 128), f32)...  105 us
    unnamed x4, local copies, waits for them, and re-layouts  4.04 us

profile of v5, /device:TPU:0, one launch (start us, length us, event | category | flops | bytes accessed | tf_op | source)
XLA Modules:
  0.0 111.4 jit_solution(13514513837324330514)
XLA Ops:
  0.6 105.4 %exits.1 = (f32[3,128]{1,0:T(4,128)}, bf16[3,16,1024]{2,1,0:T(8,128)(2,1)}, bf16[8192,512]{1,0:T(8,128)(2,1)S(1)}) custom-call(bf16[3,16,1024]{2,1,0:T(8,128)(2,1)} %hidden_hbm.1, f32[3,1024]{1,0:T(4,128)} %gain_hbm.1, f32[16,8192]{1,0:T(8,128)} %teacher_hbm.1, bf16[8192,512]{1,0:T(8,128)(2,1)} %head_hbm.1), custom_call_target="tpu_custom_call" | custom-call | tf_op jit(solution)/shard_map/exits/pallas_call | solution.py:597
  106.1 1.3 %slice_reduce_fusion = f32[3]{0:T(128)} fusion(f32[3,128]{1,0:T(4,128)} %get-tuple-element.6), kind=kLoop, calls=%fused_computation | loop fusion | bytes 24 | tf_op jit(solution)/shard_map/slice | solution.py:645
  107.4 0.0 copy-start
  107.4 3.4 %copy.9 = bf16[8192,512]{1,0:T(8,128)(2,1)} copy(bf16[8192,512]{1,0:T(8,128)(2,1)S(1)} %get-tuple-element.11) | data formatting | bytes 16777216
  110.8 0.0 copy-done
  110.8 0.6 copy.10
Async XLA Ops:
  107.4 3.4 %copy-start = (bf16[3,16,1024]{2,1,0:T(8,128)(2,1)S(1)}, bf16[3,16,1024]{2,1,0:T(8,128)(2,1)}, u32[]{:S(2)}) copy-start(bf16[3,16,1024]{2,1,0:T(8,128)(2,1)} %get-tuple-element.16) | copy-start | bytes 294916

commit v6 on v5

--- a/solution.py
+++ b/solution.py
@@ -132,13 +132,9 @@
     for k in range(1, count):
         top = jnp.maximum(top, slots[k])
     exps = jnp.zeros(top.shape, f32)
-    sums = jnp.zeros(top.shape, f32)
     for k in range(count):
-        part = slots[k]
-        exps = exps + jnp.exp(part - top)
-        sums = sums + part
-    row = lax.broadcasted_iota(jnp.int32, top.shape, 0)
-    return jnp.where(row < EXITS, top + jnp.log(exps), sums)
+        exps = exps + jnp.exp(slots[k] - top)
+    return top + jnp.log(exps)
 
 
 def kernel(
@@ -373,22 +369,24 @@
     far_blocks(turned(y, 2), 1 - xh, True, True)
     far_blocks(turned(y, 2), xh, True, False)
     lax.fori_loop(0, 3, far_step, 0)
-    for copy in lent:
-        copy.wait_recv()
 
     columns = []
     for e in range(EXITS):
         block = logits[e].reshape(TOKENS, cols)
         top = jnp.max(block, axis=1, keepdims=True)
         columns.append(top + jnp.log(jnp.sum(jnp.exp(block - top), axis=1, keepdims=True)))
+    vocab_slots[v] = jnp.transpose(by_lane(columns, TOKENS))[:8]
+    total_copies = begin(copies, vocab_slots, v, vocab_peers(s, v))
+    wait_for(lent)
     stored = target[...].reshape(TOKENS, cols)
     weight = jnp.exp(stored)
+    teacher_columns = []
     for e in range(EXITS):
         block = logits[e].reshape(TOKENS, cols)
-        columns.append(jnp.sum(weight * (stored - block), axis=1, keepdims=True))
-    columns.append(jnp.sum(weight, axis=1, keepdims=True))
-    vocab_slots[v] = jnp.transpose(by_lane(columns, TOKENS))[:8]
-    to_all(copies, vocab_slots, v, vocab_peers(s, v))
+        teacher_columns.append(jnp.sum(weight * (stored - block), axis=1, keepdims=True))
+    teacher_columns.append(jnp.sum(weight, axis=1, keepdims=True))
+    target[...] = weight.reshape(16, ROWS, cols)
+    wait_for(total_copies)
     section_slots[s] = merged(vocab_slots, 16)
     to_all(copies, section_slots, s, section_peers(s, v))
     rows = merged(section_slots, 8)
@@ -396,6 +394,7 @@
     for e in range(EXITS):
         block = logits[e].reshape(TOKENS, cols)
         log_total = turned_rows[:, e : e + 1]
+        weight = target[...].reshape(TOKENS, cols)
         grad = (jnp.exp(block - log_total) - weight) * (loss_scale / TOKENS)
         dlogit[e * TOKENS : (e + 1) * TOKENS, :] = grad.astype(bf16)
 
@@ -440,10 +439,6 @@
         )
         grad_head[head_rows(k), :] = part.astype(bf16)
         return 0
-
-    terms = rows[EXITS : 2 * EXITS] + rows[:EXITS] * rows[2 * EXITS : 2 * EXITS + 1]
-    mean = jnp.sum(terms, axis=1, keepdims=True) / TOKENS
-    divergence[...] = jnp.broadcast_to(mean, (EXITS, 128))
 
     def add(e, axis, at, whole, part, arrived):
         dims = whole_dims(whole)
@@ -531,7 +526,7 @@
     for e in range(EXITS):
         grad = dlogit[e * TOKENS : (e + 1) * TOKENS, :].astype(f32)
         columns.append(jnp.sum(grad * logits[e].reshape(TOKENS, cols), axis=1, keepdims=True))
-    inner_vocab[v] = jnp.transpose(by_lane(columns, TOKENS))[:8]
+    inner_vocab[v] = jnp.transpose(by_lane(columns + teacher_columns, TOKENS))[:8]
     inner_copies = begin(copies, inner_vocab, v, vocab_peers(s, v))
     lax.fori_loop(0, 5, fold, 0)
     wait_for(inner_copies)
@@ -556,6 +551,9 @@
         last_sums(e, ORDER[e][2], ORDER[e][:2], first[e], waits[e])
     wait_for(inner_copies)
     inner = slots_sum(inner_section, 8)
+    terms = inner[EXITS : 2 * EXITS] + rows[:EXITS] * inner[2 * EXITS : 2 * EXITS + 1]
+    for e in range(EXITS):
+        divergence[e] = jnp.sum(terms[e : e + 1, :]) / TOKENS
     inner_rows[...] = jnp.transpose(jnp.concatenate([inner, jnp.zeros((120, TOKENS), f32)], axis=0))
     second = (second_0, second_1, second_2)
     began = [first_copies(e, ORDER[e][1], ORDER[e][:1], second[e]) for e in range(EXITS)]
@@ -597,12 +595,12 @@
     divergence, grad_hidden, grad_head = pl.pallas_call(
         kernel,
         out_shape=(
-            jax.ShapeDtypeStruct((EXITS, 128), f32),
+            jax.ShapeDtypeStruct((EXITS,), f32),
             jax.ShapeDtypeStruct(exit_hidden.shape, bf16),
             pltpu.VMEM(head_weight.shape, bf16),
         ),
         in_specs=[hbm] * 4,
-        out_specs=(vmem,) * 3,
+        out_specs=(pl.BlockSpec(memory_space=pltpu.SMEM), vmem, vmem),
         scratch_shapes=[
             pltpu.VMEM(exit_hidden.shape, bf16),
             pltpu.VMEM(norm_gain.shape, f32),
@@ -642,7 +640,7 @@
         ),
         name="exits",
     )(exit_hidden, norm_gain, teacher, head_weight)
-    return divergence[:, 0], grad_hidden, grad_head
+    return divergence, grad_hidden, grad_head
 
 
 def solution(mesh):

time: 112 us -> 110 us (0.982)
    slice x1 -> x0, local copies, waits for them, and re-layouts: 1.31 us -> none  [body(): return (divergence[:, 0], grad_hidden, grad_head)]
    unnamed x4 -> x7, local copies, waits for them, and re-layouts: 4.04 us -> 4.56 us
where the time goes in v6:
time: 110 us
  Pallas kernels  105 us (95%)
  local copies, waits for them, and re-layouts  4.56 us (4%)
    pallas_call x1, Pallas kernels, body(): pl.pallas_call(kernel, out_shape=(jax.ShapeDtypeStruct((EXITS,), f32), ja...  105 us
    unnamed x7, local copies, waits for them, and re-layouts  4.56 us

profile of v6, /device:TPU:0, one launch (start us, length us, event | category | flops | bytes accessed | tf_op | source)
XLA Modules:
  0.0 110.3 jit_solution(4139718547400649674)
XLA Ops:
  0.6 105.1 %exits.1 = (f32[3]{0:T(128)}, bf16[3,16,1024]{2,1,0:T(8,128)(2,1)}, bf16[8192,512]{1,0:T(8,128)(2,1)S(1)}) custom-call(bf16[3,16,1024]{2,1,0:T(8,128)(2,1)} %hidden_hbm.1, f32[3,1024]{1,0:T(4,128)} %gain_hbm.1, f32[16,8192]{1,0:T(8,128)} %teacher_hbm.1, bf16[8192,512]{1,0:T(8,128)(2,1)} %head_hbm.1), custom_call_target="tpu_custom_call" | custom-call | tf_op jit(solution)/shard_map/exits/pallas_call | solution.py:595
  105.7 0.0 copy-start.1
  105.8 0.0 copy-start
  105.8 3.4 %copy.10 = bf16[8192,512]{1,0:T(8,128)(2,1)} copy(bf16[8192,512]{1,0:T(8,128)(2,1)S(1)} %get-tuple-element.5) | data formatting | bytes 16777216
  109.2 0.0 copy-done.1
  109.2 0.5 copy.11
  109.7 0.0 copy-done
  109.7 0.6 copy.12
Async XLA Ops:
  105.7 3.4 %copy-start.1 = (f32[3]{0:T(128)S(1)}, f32[3]{0:T(128)}, u32[]{:S(2)}) copy-start(f32[3]{0:T(128)} %get-tuple-element.9) | copy-start | bytes 40
  105.8 3.9 %copy-start = (bf16[3,16,1024]{2,1,0:T(8,128)(2,1)S(1)}, bf16[3,16,1024]{2,1,0:T(8,128)(2,1)}, u32[]{:S(2)}) copy-start(bf16[3,16,1024]{2,1,0:T(8,128)(2,1)} %get-tuple-element.10) | copy-start | bytes 294916
